TPU v7x, 128 devices: a whole 4x4x4 slice. The times are simulated.
128 devices in a mesh: gx: 8 (over z, core), gy: 16 (over x, y).
Axes of the slice: x: 4, y: 4, z: 4, core: 2. Of those that a mesh axis runs over, the one named last changes fastest.
Arguments:
- density: float32 [8, 1024, 4096], P(None, 'gy', 'gx'), may hold values from -6 to 6
- tracer: float32 [8, 1024, 4096], P(None, 'gy', 'gx'), may hold values from -6 to 6
- sea_mask: int32 [1024, 4096], P('gy', 'gx'), may hold values 0 or 1
- mixed_level: int32 [1024, 4096], P('gy', 'gx'), may hold values from 0 to 4
- tile_blocks: int32 [128], replicated, may hold values from 0 to 127, each once
- block_owner: int32 [128], replicated, may hold values from 0 to 127, as said below
Outputs:
- tracer_out: float32 [8, 1024, 4096], P(None, 'gy', 'gx')
Inputs may be any that keep to these rules, and one draw needn't show every extreme that they name: `sea_mask`: 1 marks sea, 0 land. `tile_blocks`: each of the 128 blocks once. `block_owner`: each of the 128 dynamics slots once; slot t belongs to gy index t // 8; of the 8 physics slots of one gy index, at most 2 go to any one gy index, and exactly 2 to every gy index that they reach.
All inputs are finite; a program needn't handle non-finite values. No bound on the sum of `sea_mask` on one device may be relied on, other than what follows from the above.
Results may differ from a plain program's by a relative error of at most 0.0003.
Values sent between devices are 32-bit elements; how exact they have to be, the bound alone decides.
No kernel may reach another device: no remote copies, remote signals or barrier semaphores. Data moves between devices by JAX's collectives and lax.ppermute only.
A program may use at most 128 MiB of HBM per device.

v0:
```python
import jax
import jax.numpy as jnp
from jax import lax
from jax.sharding import PartitionSpec as P

K = 8
BR = 8
BPD = 8
CAP = 2
ITERS = 4


TIME_STEP = 0.2
STRATIFICATION = 1.0
DENSITY_FLOOR = 0.25
SLOPE_LIMIT = 1.0
TAPER_WIDTH = 0.5
KERNEL_OFFSET = 0.05
BASE_DIFFUSIVITY = 0.2
VISBECK_ALPHA = 0.5


def padded(cells, sides, width):
    for axis, dim in sides:
        count = lax.axis_size(axis)
        head = lax.slice_in_dim(cells, 0, width, axis=dim)
        tail = lax.slice_in_dim(cells, cells.shape[dim] - width, cells.shape[dim], axis=dim)
        cells = jnp.concatenate(
            [
                lax.ppermute(tail, axis, [(i, (i + 1) % count) for i in range(count)]),
                cells,
                lax.ppermute(head, axis, [((i + 1) % count, i) for i in range(count)]),
            ],
            axis=dim,
        )
    return cells


def side_by_side(arrays, axis, dim, along):
    ends, at = ([], 0)
    for a in arrays[:-1]:
        at += a.shape[along]
        ends.append(at)
    both = jnp.concatenate(arrays, axis=along)
    return tuple(jnp.split(lax.all_gather(both, axis, axis=dim, tiled=True), ends, axis=along))


def interior(quantity):
    return quantity[..., 1:-1, 1:-1]


def masked_steps(quantity, seawater):
    across_east = seawater[..., :, 1:] * seawater[..., :, :-1]
    across_north = seawater[..., 1:, :] * seawater[..., :-1, :]
    step_east = (quantity[..., :, 1:] - quantity[..., :, :-1]) * across_east
    step_north = (quantity[..., 1:, :] - quantity[..., :-1, :]) * across_north
    return (step_east, step_north)


def centered_east(step_east):
    return 0.5 * (step_east[..., 1:-1, 1:] + step_east[..., 1:-1, :-1])


def centered_north(step_north):
    return 0.5 * (step_north[..., 1:, 1:-1] + step_north[..., :-1, 1:-1])


def vertical_center(quantity):
    shallower = jnp.concatenate([quantity[:1], quantity[:-1]], axis=0)
    deeper = jnp.concatenate([quantity[1:], quantity[-1:]], axis=0)
    return 0.5 * (deeper - shallower)


def vertical_divergence(column_flux):
    zero_layer = jnp.zeros_like(column_flux[:1])
    shallower = jnp.concatenate([zero_layer, column_flux[:-1]], axis=0)
    deeper = jnp.concatenate([column_flux[1:], zero_layer], axis=0)
    return 0.5 * (deeper - shallower)


def physics(density_rim, seawater_rim, mixed_depth):
    level_count = density_rim.shape[0]
    levels = jnp.arange(level_count, dtype=jnp.float32).reshape(-1, 1, 1, 1)
    step_east, step_north = masked_steps(density_rim, seawater_rim)
    grad_east = centered_east(step_east)
    grad_north = centered_north(step_north)
    stratified = vertical_center(interior(density_rim) + STRATIFICATION * levels)
    denominator = jnp.maximum(stratified, DENSITY_FLOOR)
    slope_east = -grad_east / denominator
    slope_north = -grad_north / denominator
    squared = slope_east * slope_east + slope_north * slope_north
    taper_factor = 0.5 * (1.0 + jnp.tanh((SLOPE_LIMIT - squared) / TAPER_WIDTH))
    surface = jnp.minimum(1.0, (levels + 1.0) / (mixed_depth + 1.0))
    seawater = interior(seawater_rim)
    factor = taper_factor * surface * seawater
    slope_east = slope_east * factor
    slope_north = slope_north * factor
    tapered_sq = slope_east * slope_east + slope_north * slope_north
    below_layer = (levels >= mixed_depth).astype(jnp.float32)
    kernel = jnp.sqrt(denominator * (tapered_sq + KERNEL_OFFSET)) * below_layer
    depth_count = level_count - mixed_depth
    diffusivity = seawater * (
        BASE_DIFFUSIVITY + VISBECK_ALPHA * jnp.sum(kernel, axis=0) / depth_count
    )
    return (slope_east, slope_north, diffusivity)


def advance(tracer_rim, east_rim, north_rim, diffusivity_rim, seawater_rim):
    step_east, step_north = masked_steps(tracer_rim, seawater_rim)
    face_east = 0.5 * (diffusivity_rim[..., :, 1:] + diffusivity_rim[..., :, :-1]) * step_east
    face_north = 0.5 * (diffusivity_rim[..., 1:, :] + diffusivity_rim[..., :-1, :]) * step_north
    lateral = (
        face_east[..., 1:-1, 1:]
        - face_east[..., 1:-1, :-1]
        + (face_north[..., 1:, 1:-1] - face_north[..., :-1, 1:-1])
    )
    grad_east = centered_east(step_east)
    grad_north = centered_north(step_north)
    center_tracer = interior(tracer_rim)
    grad_down = vertical_center(center_tracer)
    slope_east = interior(east_rim)
    slope_north = interior(north_rim)
    column_flux = interior(diffusivity_rim) * (
        2.0 * slope_east * grad_east
        + 2.0 * slope_north * grad_north
        + (slope_east * slope_east + slope_north * slope_north) * grad_down
    )
    tendency = (lateral + vertical_divergence(column_flux)) * interior(seawater_rim)
    return center_tracer + TIME_STEP * tendency


def extend(quantity, blocks_of_slot, width):
    widened = padded(quantity, (("gx", 2),), width)
    channels = quantity.shape[0]
    blocks = widened.reshape(channels, BPD, BR, widened.shape[-1])
    top_rows = blocks[:, :, :width]
    bottom_rows = blocks[:, :, BR - width :]
    every_top, every_bottom = side_by_side((top_rows, bottom_rows), "gy", 1, 0)
    block_count = blocks_of_slot.shape[0]
    slot_of_block = jnp.argsort(blocks_of_slot)
    own_slots = lax.axis_index("gy") * BPD + jnp.arange(BPD, dtype=jnp.int32)
    global_ids = jnp.take(blocks_of_slot, own_slots)
    slot_above = jnp.take(slot_of_block, jnp.clip(global_ids - 1, 0, block_count - 1))
    slot_below = jnp.take(slot_of_block, jnp.clip(global_ids + 1, 0, block_count - 1))
    has_above = (global_ids > 0).astype(jnp.float32)[None, :, None, None]
    has_below = (global_ids < block_count - 1).astype(jnp.float32)[None, :, None, None]
    upper_rows = jnp.take(every_bottom, slot_above, axis=1) * has_above
    lower_rows = jnp.take(every_top, slot_below, axis=1) * has_below
    return jnp.concatenate([upper_rows, blocks, lower_rows], axis=2)


def relay_plan(block_owner):
    devices = block_owner.shape[0] // BPD
    own_index = lax.axis_index("gy")
    owners = (block_owner // BPD).reshape(devices, BPD)
    position = jnp.arange(BPD, dtype=jnp.int32)
    earlier_same = (owners[:, :, None] == owners[:, None, :]) & (
        position[:, None] < position[None, :]
    )[None]
    sender_rank = jnp.sum(earlier_same.astype(jnp.int32), axis=1)
    my_owners = jnp.take(owners, own_index, axis=0)
    my_rank = jnp.take(sender_rank, own_index, axis=0)
    slot_codes = my_owners * CAP + my_rank
    buffer_slots = jnp.arange(devices * CAP, dtype=jnp.int32)
    slot_hits = (slot_codes[None, :] == buffer_slots[:, None]).astype(jnp.int32)
    send_index = jnp.sum(slot_hits * position[None, :], axis=1)
    source_slots = jnp.take(jnp.argsort(block_owner), own_index * BPD + position)
    receive_index = source_slots // BPD * CAP + jnp.take(sender_rank.reshape(-1), source_slots)
    return (send_index, receive_index)


def on_device(density, tracer, sea_mask, mixed_level, tile_blocks, block_owner):
    row_count = density.shape[1]
    column_count = density.shape[2]
    dynamics_blocks = jnp.take(tile_blocks, jnp.argsort(block_owner))
    send_index, receive_index = relay_plan(block_owner)
    seawater_flat = sea_mask.astype(jnp.float32)
    depth_flat = mixed_level.astype(jnp.float32)
    package = jnp.concatenate([density, seawater_flat[None], depth_flat[None]], axis=0).reshape(
        K + 2, BPD, BR, column_count
    )
    outgoing = jnp.take(package, send_index, axis=1)
    arrived = jnp.take(
        lax.all_to_all(outgoing, "gy", split_axis=1, concat_axis=1, tiled=True),
        receive_index,
        axis=1,
    )
    bordered = extend(arrived[: K + 1].reshape(K + 1, row_count, column_count), dynamics_blocks, 1)
    slope_east, slope_north, diffusivity = physics(bordered[:K], bordered[K], arrived[K + 1])
    seawater = interior(bordered[K])
    current = tracer
    statics = extend(
        jnp.stack([diffusivity, seawater]).reshape(2, row_count, column_count), dynamics_blocks, 1
    )
    margin = ((0, 0), (0, 0), (1, 1), (1, 1))
    east_rim = jnp.pad(slope_east, margin)
    north_rim = jnp.pad(slope_north, margin)
    for sweep_index in range(ITERS):
        advanced = advance(
            extend(current, dynamics_blocks, 1), east_rim, north_rim, statics[0], statics[1]
        )
        current = advanced.reshape(K, row_count, column_count)
    return current


def solution(mesh):
    placed = (P(None, "gy", "gx"), P(None, "gy", "gx"), P("gy", "gx"), P("gy", "gx"), P(), P())
    return jax.shard_map(
        on_device, mesh=mesh, in_specs=placed, out_specs=P(None, "gy", "gx"), check_vma=False
    )
```

profile of v0, /device:TPU:32, one launch (start us, length us, event | category | flops | bytes accessed | tf_op | source)
XLA Modules:
  0.0 608.4 jit_solution(13675218678553005191)
XLA Ops:
  10.2 3.2 gather_fusion
  13.4 5.9 select_bitcast_fusion
  19.3 7.2 %all-to-all-start = ((f32[10,32,8,512]{3,2,0,1:T(8,128)}), f32[10,32,8,512]{3,2,0,1:T(8,128)}, u32[]{:S(2)}, u32[]{:S(2)}) async-start(f32[10,32,8,512]{3,2,0,1:T(8,128)} %select_bitcast_fusion), calls=%async_computation | async-start | bytes 10485760 | tf_op jit(solution)/shard_map/all_to_all | solution.py:184
  32.6 72.8 %all-to-all-done = f32[10,32,8,512]{3,2,0,1:T(8,128)} async-done(((f32[10,32,8,512]{3,2,0,1:T(8,128)}), f32[10,32,8,512]{3,2,0,1:T(8,128)}, u32[]{:S(2)}, u32[]{:S(2)}) %all-to-all-start) | async-done | bytes 5242912 | tf_op jit(solution)/shard_map/all_to_all | solution.py:184
  105.3 5.6 copy.284
  111.0 3.1 gather_fusion.1
  115.4 3.5 collective-permute-done.3
  124.6 3.9 collective-permute-done.1
  145.1 46.4 %all-gather.7.cloned.1.call-done = f32[18,128,1,514]{3,2,0,1:T(1,128)} async-done(((f32[18,8,1,514]{3,2,0,1:T(1,128)}), f32[18,128,1,514]{3,2,0,1:T(1,128)}) %all-gather.7.cloned.1.call-update) | async-done | bytes 4737040 | tf_op jit(solution)/shard_map/all_gather | solution.py:45
  191.5 6.8 %fusion.109 = (f32[9,128,1,514]{3,2,0,1:T(1,128)S(1)}, f32[9,128,1,514]{3,2,0,1:T(1,128)S(1)}) fusion(f32[18,128,1,514]{3,2,0,1:T(1,128)} %all-gather.7.cloned.1.call-done), kind=kLoop, calls=%fused_computation.294 | loop fusion | bytes 9474048 | tf_op jit(solution)/shard_map/split | solution.py:45
  203.9 4.0 gather_fusion.9
  207.9 4.0 gather_fusion.7
  228.2 15.6 %fusion.112 = (f32[7,8,8,512]{3,2,0,1:T(8,128)}, f32[7,8,8,512]{3,2,0,1:T(8,128)}) fusion(f32[8,64,1]{2,1,0:T(8,128)S(1)} %collective-permute-done.1, f32[8,64,512]{2,1,0:T(8,128)S(1)} %copy-done.2, f32[8,64,1]{2,1,0:T(8,128)} %copy-done.13), kind=kLoop, calls=%fused_computation.297 | loop fusion | flops 526336 | bytes 2887680 | tf_op jit(solution)/shard_map/slice | solution.py:69
  244.9 4.5 all-gather.11.cloned.1.call-done
  249.5 6.1 %fusion.110 = (f32[8,128,1,514]{3,2,1,0:T(1,128)S(1)}, f32[8,128,1,514]{3,2,1,0:T(1,128)S(1)}) fusion(f32[16,128,1,514]{3,2,1,0:T(1,128)} %all-gather.11.cloned.1.call-done), kind=kLoop, calls=%fused_computation.295 | loop fusion | bytes 8421376 | tf_op jit(solution)/shard_map/split | solution.py:45
  255.6 5.3 copy_bitcast_fusion.2
  260.9 3.1 gather_fusion.13
  270.1 3.2 pad_maximum_fusion.7
  273.3 21.2 %all-gather.9.cloned.1.call-done = f32[4,128,1,514]{3,2,1,0:T(1,128)} async-done(((f32[4,8,1,514]{3,2,1,0:T(1,128)}), f32[4,128,1,514]{3,2,1,0:T(1,128)}) %all-gather.9.cloned.1.call-update) | async-done | bytes 1052688 | tf_op jit(solution)/shard_map/all_gather | solution.py:45
  294.4 3.2 fusion.114
  317.4 17.3 %fusion.60 = f32[8,8,8,512]{3,2,0,1:T(8,128)S(1)} fusion(f32[8,8,9,514]{3,2,0,1:T(8,128)S(1)} %get-tuple-element.62, f32[8,8,10,513]{3,2,0,1:T(8,128)S(1)} %get-tuple-element.31, f32[7,8,8,512]{3,2,0,1:T(8,128)S(1)} %get-tuple-element.98, f32[7,8,8,512]{3,2,0,1:T(8,128)S(1)} %get-tuple-element.97, f32[8,8,512]{2,1,0:T(8,128)S(1)} %slice.691, ...), kind=kLoop, calls=%fused_computation.139 | loop fusion | flops 2885632 | bytes 8261632 | tf_op jit(solution)/shard_map/add | solution.py:129
  335.5 3.4 collective-permute-done.7
  345.4 53.6 %all-gather.13.cloned.1.call-done = f32[16,128,1,514]{3,0,2,1:T(8,128)} async-done(((f32[16,8,1,514]{3,0,2,1:T(8,128)}), f32[16,128,1,514]{3,0,2,1:T(8,128)}) %all-gather.13.cloned.1.call-update) | async-done | bytes 4210704 | tf_op jit(solution)/shard_map/all_gather | solution.py:45
  399.0 5.2 slice_bitcast_fusion.4
  422.5 3.4 collective-permute-done.9
  432.6 54.6 %all-gather.15.cloned.1.call-done = f32[16,128,1,514]{3,0,2,1:T(8,128)} async-done(((f32[16,8,1,514]{3,0,2,1:T(8,128)}), f32[16,128,1,514]{3,0,2,1:T(8,128)}) %all-gather.15.cloned.1.call-update) | async-done | bytes 4210704 | tf_op jit(solution)/shard_map/all_gather | solution.py:45
  487.1 5.2 slice_bitcast_fusion.2
  496.5 3.1 gather_fusion.16
  511.8 3.4 collective-permute-done.11
  521.9 54.5 %all-gather.17.cloned.1.call-done = f32[16,128,1,514]{3,0,2,1:T(8,128)} async-done(((f32[16,8,1,514]{3,0,2,1:T(8,128)}), f32[16,128,1,514]{3,0,2,1:T(8,128)}) %all-gather.17.cloned.1.call-update) | async-done | bytes 4210704 | tf_op jit(solution)/shard_map/all_gather | solution.py:45
  576.4 5.2 slice_bitcast_fusion
  590.7 3.2 fusion.10
  (351 shorter events, 152.5 us)
Async XLA Ops:
  6.5 23.3 %copy-start = (s32[128]{0:T(128)S(1)}, s32[128]{0:T(128)}, u32[]{:S(2)}) copy-start(s32[128]{0:T(128)} %param.20) | copy-start | bytes 1540
  19.3 86.1 %all-to-all-start = ((f32[10,32,8,512]{3,2,0,1:T(8,128)}), f32[10,32,8,512]{3,2,0,1:T(8,128)}, u32[]{:S(2)}, u32[]{:S(2)}) async-start(f32[10,32,8,512]{3,2,0,1:T(8,128)} %select_bitcast_fusion), calls=%async_computation | async-start | bytes 10485760 | tf_op jit(solution)/shard_map/all_to_all | solution.py:184
  26.5 165.0 %all-gather.7.cloned.1.call-start = ((), (), s32[]{:S(2)}) async-start(), calls=%async_computation.1 | async-start | bytes 6266880 | tf_op jit(solution)/shard_map/all_gather | solution.py:45
  114.6 4.3 collective-permute-start.3
  114.7 6.2 %collective-permute-start.2 = (f32[9,64,1]{2,1,0:T(8,128)S(1)}, f32[9,64,1]{2,1,0:T(8,128)S(1)}, u32[]{:S(2)}, u32[]{:S(2)}) collective-permute-start(f32[9,64,1]{2,1,0:T(8,128)S(1)} %get-tuple-element.71), channel_id=1, source_target_pairs={{0,16},{16,32},{32,48},{48,64},{64,80},{80,96},{96,112},{112,0},{1... | collective-permute-start | bytes 6920 | tf_op jit(solution)/shard_map/ppermute | solution.py:30
  123.4 126.1 %all-gather.11.cloned.1.call-start = ((), (), s32[]{:S(2)}) async-start(), calls=%async_computation.3 | async-start | bytes 5570560 | tf_op jit(solution)/shard_map/all_gather | solution.py:45
  123.6 4.9 collective-permute-start.1
  124.6 6.1 %collective-permute-start = (f32[8,64,1]{2,1,0:T(8,128)S(1)}, f32[8,64,1]{2,1,0:T(8,128)S(1)}, u32[]{:S(2)}, u32[]{:S(2)}) collective-permute-start(f32[8,64,1]{2,1,0:T(8,128)S(1)} %get-tuple-element.99), channel_id=1, source_target_pairs={{0,16},{16,32},{32,48},{48,64},{64,80},{80,96},{96,112},{112,0},{1... | collective-permute-start | bytes 6152 | tf_op jit(solution)/shard_map/ppermute | solution.py:30
  132.5 162.0 %all-gather.9.cloned.1.call-start = ((), (), s32[]{:S(2)}) async-start(), calls=%async_computation.2 | async-start | bytes 1392640 | tf_op jit(solution)/shard_map/all_gather | solution.py:45
  201.1 13.3 %copy-start.32 = (f32[9,8,8,1]{3,2,0,1:T(8,128)S(1)}, f32[9,8,8,1]{3,2,0,1:T(8,128)}, u32[]{:S(2)}) copy-start(f32[9,8,8,1]{3,2,0,1:T(8,128)} %copy-done.31) | copy-start | bytes 6916
  201.1 13.3 %copy-start.34 = (f32[9,8,8,1]{3,2,0,1:T(8,128)S(1)}, f32[9,8,8,1]{3,2,0,1:T(8,128)}, u32[]{:S(2)}) copy-start(f32[9,8,8,1]{3,2,0,1:T(8,128)} %copy-done.33) | copy-start | bytes 6916
  221.1 94.2 %copy-start.3 = (f32[8,8,8,512]{3,2,0,1:T(8,128)}, f32[8,8,8,512]{3,2,0,1:T(8,128)S(1)}, u32[]{:S(2)}) copy-start(f32[8,8,8,512]{3,2,0,1:T(8,128)S(1)} %get-tuple-element.35) | copy-start | bytes 3145732
  222.4 1.9 collective-permute-start.5
  222.4 3.7 collective-permute-start.4
  227.8 171.2 %all-gather.13.cloned.1.call-start = ((), (), s32[]{:S(2)}) async-start(), calls=%async_computation.4 | async-start | bytes 5570560 | tf_op jit(solution)/shard_map/all_gather | solution.py:45
  228.2 15.6 %copy-start.14 = (f32[8,64,1]{2,1,0:T(8,128)S(1)}, f32[8,64,1]{2,1,0:T(8,128)}, u32[]{:S(2)}) copy-start(f32[8,64,1]{2,1,0:T(8,128)} %copy-done.13) | copy-start | bytes 6148
  313.1 107.7 %copy-start.48 = (f32[8,8,512]{2,1,0:T(8,128)}, f32[8,8,512]{2,1,0:T(8,128)S(1)}, u32[]{:S(2)}) copy-start(f32[8,8,512]{2,1,0:T(8,128)S(1)} %slice.691) | copy-start | bytes 393220
  335.0 3.9 collective-permute-start.7
  335.0 5.8 collective-permute-start.6
  343.1 144.0 %all-gather.15.cloned.1.call-start = ((), (), s32[]{:S(2)}) async-start(), calls=%async_computation.5 | async-start | bytes 5570560 | tf_op jit(solution)/shard_map/all_gather | solution.py:45
  345.4 67.8 %copy-start.24 = (f32[8,9,514]{2,1,0:T(8,128)S(1)}, f32[8,9,514]{2,1,0:T(8,128)}, u32[]{:S(2)}) copy-start(f32[8,9,514]{2,1,0:T(8,128)} %copy-done.23) | copy-start | bytes 444100
  345.4 67.8 %copy-start.28 = (f32[8,9,514]{2,1,0:T(8,128)S(1)}, f32[8,9,514]{2,1,0:T(8,128)}, u32[]{:S(2)}) copy-start(f32[8,9,514]{2,1,0:T(8,128)} %copy-done.27) | copy-start | bytes 444100
  422.0 3.9 collective-permute-start.9
  422.0 5.8 collective-permute-start.8
  428.5 72.3 %copy-start.37 = (f32[8,8,8,1]{3,2,0,1:T(8,128)}, f32[8,8,8,1]{3,2,0,1:T(8,128)S(1)}, u32[]{:S(2)}) copy-start(f32[8,8,8,1]{3,2,0,1:T(8,128)S(1)} %copy.325) | copy-start | bytes 6148
  430.2 146.2 %all-gather.17.cloned.1.call-start = ((), (), s32[]{:S(2)}) async-start(), calls=%async_computation.6 | async-start | bytes 5570560 | tf_op jit(solution)/shard_map/all_gather | solution.py:45
  432.6 68.3 %copy-start.25 = (f32[8,9,514]{2,1,0:T(8,128)S(1)}, f32[8,9,514]{2,1,0:T(8,128)}, u32[]{:S(2)}) copy-start(f32[8,9,514]{2,1,0:T(8,128)} %copy-done.23) | copy-start | bytes 444100
  432.6 68.3 %copy-start.29 = (f32[8,9,514]{2,1,0:T(8,128)S(1)}, f32[8,9,514]{2,1,0:T(8,128)}, u32[]{:S(2)}) copy-start(f32[8,9,514]{2,1,0:T(8,128)} %copy-done.27) | copy-start | bytes 444100
  511.2 3.9 collective-permute-start.11
  511.2 6.0 collective-permute-start.10
  521.9 68.8 %copy-start.26 = (f32[8,9,514]{2,1,0:T(8,128)S(1)}, f32[8,9,514]{2,1,0:T(8,128)}, u32[]{:S(2)}) copy-start(f32[8,9,514]{2,1,0:T(8,128)} %copy-done.23) | copy-start | bytes 444100
  521.9 68.8 %copy-start.30 = (f32[8,9,514]{2,1,0:T(8,128)S(1)}, f32[8,9,514]{2,1,0:T(8,128)}, u32[]{:S(2)}) copy-start(f32[8,9,514]{2,1,0:T(8,128)} %copy-done.27) | copy-start | bytes 444100
  (62 other events, 133.5 us)
Sparse Core Ops, SparseCore 0:
  123.5 68.0 all-gather.6
  193.7 55.6 all-gather.10
  251.7 42.7 all-gather.8
  343.3 55.6 all-gather.12
  430.3 56.7 all-gather.14
  519.7 56.6 all-gather.16
where the time goes:
time: 616 us; the launch traced here: 608 us
  waiting for transfers between devices  336 us (55%)
  local copies, waits for them, and re-layouts  134 us (22%)
  other arithmetic  112 us (18%)
  between operations  15.3 us (2%)
  starting transfers between devices  11.7 us (2%)
    all_gather x6, waiting for transfers between devices, side_by_side(): lax.all_gather(both, axis, axis=dim, tiled=True)  235 us
    all_to_all x1, waiting for transfers between devices, on_device(): lax.all_to_all(outgoing, 'gy', split_axis=1, concat_axis=1, tiled=True)  72.8 us
    another operation x6, local copies, waits for them, and re-layouts, extend(): lower_rows = jnp.take(every_top, slot_below, axis=1) * has_below  25.7 us
    split x5, local copies, waits for them, and re-layouts, side_by_side(): jnp.split(lax.all_gather(both, axis, axis=dim, tiled=True), ends, axis=al...  20.2 us
    add x3, other arithmetic, advance(): return center_tracer + TIME_STEP * tendency  19.3 us
    ppermute x6, waiting for transfers between devices, padded(): lax.ppermute(head, axis, [((i + 1) % count, i) for i in range(count)])  18.9 us
    gather x6, local copies, waits for them, and re-layouts, extend(): upper_rows = jnp.take(every_bottom, slot_above, axis=1) * has_above  18.2 us
    gather x6, local copies, waits for them, and re-layouts, extend(): lower_rows = jnp.take(every_top, slot_below, axis=1) * has_below  18.2 us
  transfers between devices with their start and end apart: 19, of which 19 were waited for; matrix products, arithmetic and copies ran while one was open for 17% of the time, Pallas kernels for 0%

commit v1 on v0

v1 whole, which is shorter than its diff:
```python
import jax
import jax.numpy as jnp
from jax import lax
from jax.experimental import pallas as pl
from jax.experimental.pallas import tpu as pltpu
from jax.sharding import PartitionSpec as P

K = 8
BR = 8
ITERS = 4
HALO = ITERS + 1
LANES = 128
SLOTS = 3
GROUPS = 3
VREGS = 6

TIME_STEP = 0.2
STRATIFICATION = 1.0
DENSITY_FLOOR = 0.25
SLOPE_LIMIT = 1.0
TAPER_WIDTH = 0.5
KERNEL_OFFSET = 0.05
BASE_DIFFUSIVITY = 0.2
VISBECK_ALPHA = 0.5


def rolled(x, shift):
    shift %= LANES
    return x if shift == 0 else pltpu.roll(x, shift, x.ndim - 1)


def lane_of(shape=(BR, LANES)):
    return lax.broadcasted_iota(jnp.int32, shape, len(shape) - 1)


def plane_at(register, piece):
    if piece == 2 and register == 2:
        return 2 * K
    if piece == 2 and register == 5:
        return 2 * K + 1
    return register % 3 + 3 * piece + (K if register >= 3 else 0)


def edges_kernel(d_first, d_last, t_first, t_last, s_first, s_last, m_first, m_last, head_ref, tail_ref):
    shape = (d_first.shape[1], LANES)
    lane = lane_of(shape)

    def gather(density, tracer, mask, mixed, start):
        out = jnp.zeros(shape, jnp.float32)
        for p in range(2 * K + 2):
            if p < K:
                plane = density[p]
            elif p < 2 * K:
                plane = tracer[p - K]
            else:
                plane = (mask if p == 2 * K else mixed)[...].astype(jnp.float32)
            at = HALO * p
            out = jnp.where((lane >= at) & (lane < at + HALO), rolled(plane, at - start), out)
        return out

    head_ref[...] = gather(d_first, t_first, s_first, m_first, 0)
    tail_ref[...] = gather(d_last, t_last, s_last, m_last, LANES - HALO)


def edges(density, tracer, mask, mixed):
    rows, columns = mask.shape
    last = columns // LANES - 1
    cube = lambda c: pl.BlockSpec((K, rows, LANES), lambda i: (0, 0, c))
    flat = lambda c: pl.BlockSpec((rows, LANES), lambda i: (0, c))
    out = jax.ShapeDtypeStruct((rows, LANES), jnp.float32)
    rim = pl.BlockSpec((rows, LANES), lambda i: (0, 0))
    return pl.pallas_call(
        edges_kernel,
        grid=(1,),
        out_shape=(out, out),
        out_specs=(rim, rim),
        in_specs=[cube(0), cube(last), cube(0), cube(last), flat(0), flat(last), flat(0), flat(last)],
        name="edges",
    )(density, density, tracer, tracer, mask, mask, mixed, mixed)


def pack_kernel(width, density, tracer, mask, mixed, out_ref):
    piece = width + 2 * HALO
    per_tile = LANES // width
    tiles = mask.shape[1] // LANES
    lane = lane_of()

    def columns(p):
        for t in range(tiles):
            at = slice(LANES * t, LANES * (t + 1))
            if p < K:
                yield density[p, :, at]
            elif p < 2 * K:
                yield tracer[p - K, :, at]
            else:
                yield (mask if p == 2 * K else mixed)[:, at].astype(jnp.float32)

    for v in range(VREGS):
        whole, seam = [], []
        for m in range(SLOTS):
            own = list(columns(plane_at(v, m)))
            whole.append(own)
            seam.append(
                [own[0]]
                + [jnp.where(lane < LANES // 2, own[t], own[t - 1]) for t in range(1, tiles)]
                + [own[-1]]
            )
        for j in range(tiles * per_tile):
            t, q = divmod(j, per_tile)
            parts = []
            for m in range(SLOTS):
                if q == 0:
                    source = seam[m][t]
                elif q == per_tile - 1:
                    source = seam[m][t + 1]
                else:
                    source = whole[m][t]
                parts.append(rolled(source, piece * m - (width * q - HALO)))
            out_ref[j, v] = jnp.where(
                lane < piece, parts[0], jnp.where(lane < 2 * piece, parts[1], parts[2])
            )


def pack(density, tracer, mask, mixed, strips):
    rows, columns = mask.shape
    blocks = rows // BR
    width = columns // strips
    cube = pl.BlockSpec((K, BR, columns), lambda b: (0, b, 0))
    flat = pl.BlockSpec((BR, columns), lambda b: (b, 0))

    def kernel(*refs):
        pack_kernel(width, *refs)

    return pl.pallas_call(
        kernel,
        grid=(blocks,),
        out_shape=jax.ShapeDtypeStruct((strips, blocks * VREGS, BR, LANES), jnp.float32),
        in_specs=[cube, cube, flat, flat],
        out_specs=pl.BlockSpec((strips, VREGS, BR, LANES), lambda b: (0, b, 0, 0)),
        cost_estimate=pl.CostEstimate(flops=20000000, bytes_accessed=6000000, transcendentals=0),
        name="pack",
    )(density, tracer, mask, mixed)


def patch_kernel(piece, west, east, packed, out_ref):
    lane = lane_of()
    blocks = west.shape[0] // BR

    def fill(edge, start):
        for b in range(blocks):
            rim = edge[BR * b : BR * (b + 1), :]
            for v in range(VREGS):
                value = packed[0, b * VREGS + v]
                for m in range(SLOTS):
                    at = piece * m + start
                    here = (lane >= at) & (lane < at + HALO)
                    value = jnp.where(here, rolled(rim, at - HALO * plane_at(v, m)), value)
                out_ref[0, b * VREGS + v] = value

    pl.when(pl.program_id(0) == 0)(lambda: fill(west, 0))
    pl.when(pl.program_id(0) == 1)(lambda: fill(east, piece - HALO))


def patch(west, east, packed, piece):
    strips, count = packed.shape[:2]
    rim = pl.BlockSpec(west.shape, lambda i: (0, 0))
    ends = pl.BlockSpec((1, count, BR, LANES), lambda i: (i * (strips - 1), 0, 0, 0))

    def kernel(*refs):
        patch_kernel(piece, *refs)

    return pl.pallas_call(
        kernel,
        grid=(2,),
        out_shape=jax.ShapeDtypeStruct(packed.shape, jnp.float32),
        in_specs=[rim, rim, ends],
        out_specs=ends,
        input_output_aliases={2: 0},
        name="patch",
    )(west, east, packed)


def sweep_kernel(
    width, blocks, order, owner, got, out_ref, slot_of, rho, sea, ta, tb, cp, cq, cr, kap, ce, cw, cn, me, mw
):
    piece = width + 2 * HALO
    lane = lane_of()
    first = lane < piece
    second = lane < 2 * piece
    slot = jnp.where(first, 0, jnp.where(second, 1, 2))
    zeros = jnp.zeros((BR, LANES), jnp.float32)

    def invert(s, carry):
        slot_of[order[s]] = s
        return carry

    lax.fori_loop(0, blocks, invert, 0)

    for edge in (0, BR * (blocks + 1)):
        for g in range(GROUPS):
            rho[g, pl.ds(edge, BR), :] = zeros
            ta[g, pl.ds(edge, BR), :] = zeros
            tb[g, pl.ds(edge, BR), :] = zeros
        sea[pl.ds(edge, BR), :] = zeros
        kap[pl.ds(edge, BR), :] = zeros
        cn[pl.ds(edge, BR), :] = zeros

    def spread(x):
        return jnp.where(first, rolled(x, -2 * piece), jnp.where(second, rolled(x, -piece), x))

    def loop(body, step=1):
        def some(i, carry):
            for u in range(step):
                body(i * step + u)
            return carry

        lax.fori_loop(0, blocks // step, some, 0)

    def rows(b, off=0):
        if off == 0:
            return pl.ds(pl.multiple_of(BR * (b + 1), BR), BR)
        return pl.ds(BR * (b + 1) + off, BR)

    def gather(b):
        s = slot_of[b]
        t = owner[s]
        for g in range(GROUPS):
            rho[g, rows(b), :] = got[s, g]
            ta[g, rows(b), :] = got[t, GROUPS + g]
        sea[rows(b), :] = spread(got[s, 2])

    loop(gather, 2)

    def deltas(f):
        f0, f1, f2 = f
        f2 = jnp.where(second, f2, f1)
        above0 = jnp.where(first, f0, rolled(f2, piece))
        return (f1 - above0, f2 - f0, rolled(f0, -piece) - f1)

    def physics(b):
        s = slot_of[b]
        mixed = spread(got[s, 5])
        here = sea[rows(b), :]
        north = sea[rows(b, 1), :] * here
        south = sea[rows(b, -1), :] * here
        east = rolled(here, -1) * here
        west = rolled(east, 1)
        me[rows(b), :] = east
        mw[rows(b), :] = west
        f = [rho[g, rows(b), :] for g in range(GROUPS)]
        down = deltas(f)
        per_mixed = 1.0 / (mixed + 1.0)
        total = zeros
        kept = []
        for g in range(GROUPS):
            level = (slot * 3 + g).astype(jnp.float32)
            step = rolled(f[g], -1) - f[g]
            sum_e = east * step + west * rolled(step, 1)
            sum_n = north * (rho[g, rows(b, 1), :] - f[g]) + south * (f[g] - rho[g, rows(b, -1), :])
            rising = jnp.where((level == 0.0) | (level == K - 1.0), 0.5 * STRATIFICATION, STRATIFICATION)
            denominator = jnp.maximum(0.5 * down[g] + rising, DENSITY_FLOOR)
            scale = -0.5 / denominator
            se = sum_e * scale
            sn = sum_n * scale
            squared = se * se + sn * sn
            taper = 0.5 + 0.5 * jnp.tanh((SLOPE_LIMIT - squared) * (1.0 / TAPER_WIDTH))
            factor = taper * jnp.minimum(1.0, (level + 1.0) * per_mixed) * here
            se = se * factor
            sn = sn * factor
            squared = se * se + sn * sn
            below = (level >= mixed) & (level < K)
            total += jnp.where(below, jnp.sqrt(denominator * (squared + KERNEL_OFFSET)), 0.0)
            kept.append((se, sn, squared))
        total = total + rolled(total, -piece) + rolled(total, -2 * piece)
        total = jnp.where(first, total, jnp.where(second, rolled(total, piece), rolled(total, 2 * piece)))
        kappa = here * (BASE_DIFFUSIVITY + VISBECK_ALPHA * total / (K - mixed))
        kap[rows(b), :] = kappa
        weight = (0.5 * TIME_STEP) * kappa
        for g in range(GROUPS):
            se, sn, squared = kept[g]
            w = jnp.where(second, weight, 0.0) if g == 2 else weight
            cp[g, rows(b), :] = w * se
            cq[g, rows(b), :] = w * sn
            cr[g, rows(b), :] = (0.5 * w) * squared

    loop(physics)

    def faces(b):
        kappa = kap[rows(b), :]
        here = sea[rows(b), :]
        east = (0.5 * TIME_STEP) * (kappa + rolled(kappa, -1)) * me[rows(b), :]
        ce[rows(b), :] = east
        cw[rows(b), :] = rolled(east, 1)
        cn[rows(b), :] = (0.5 * TIME_STEP) * (kappa + kap[rows(b, 1), :]) * (here * sea[rows(b, 1), :])

    loop(faces, 2)

    def advance(b, source):
        here = sea[rows(b), :]
        north = sea[rows(b, 1), :] * here
        south = sea[rows(b, -1), :] * here
        east = me[rows(b), :]
        west = mw[rows(b), :]
        face_e = ce[rows(b), :]
        face_w = cw[rows(b), :]
        face_n = cn[rows(b), :]
        face_s = cn[rows(b, -1), :]
        f = [source[g, rows(b), :] for g in range(GROUPS)]
        down = deltas(f)
        flux, result = [], []
        for g in range(GROUPS):
            step_e = rolled(f[g], -1) - f[g]
            step_w = rolled(step_e, 1)
            step_n = source[g, rows(b, 1), :] - f[g]
            step_s = f[g] - source[g, rows(b, -1), :]
            sum_e = east * step_e + west * step_w
            sum_n = north * step_n + south * step_s
            lateral = (face_e * step_e - face_w * step_w) + (face_n * step_n - face_s * step_s)
            flux.append(
                cp[g, rows(b), :] * sum_e + cq[g, rows(b), :] * sum_n + cr[g, rows(b), :] * down[g]
            )
            result.append(f[g] + lateral)
        result[0] += flux[1] - rolled(flux[2], piece)
        result[1] += flux[2] - flux[0]
        result[2] += rolled(flux[0], -piece) - flux[1]
        return result

    def sweep(source, target):
        def body(b):
            result = advance(b, source)
            for g in range(GROUPS):
                target[g, rows(b), :] = result[g]

        loop(body)

    sweep(ta, tb)
    sweep(tb, ta)
    sweep(ta, tb)

    per_out = LANES // width

    def last(b):
        result = advance(b, tb)
        t = owner[slot_of[b]]
        for h in range(K // per_out):
            value = None
            for m in range(per_out):
                k = h * per_out + m
                part = rolled(result[k % 3], width * m - (piece * (k // 3) + HALO))
                value = part if m == 0 else jnp.where(lane < width * m, value, part)
            out_ref[t, h] = value

    loop(last)


def sweeps(order, owner, got, width):
    blocks = got.shape[0]
    padded = BR * (blocks + 2)
    cube = pltpu.VMEM((GROUPS, padded, LANES), jnp.float32)
    flat = pltpu.VMEM((padded, LANES), jnp.float32)
    outs = K * width // LANES

    def kernel(*refs):
        sweep_kernel(width, blocks, *refs)

    return pl.pallas_call(
        kernel,
        out_shape=jax.ShapeDtypeStruct((blocks, outs, BR, LANES), jnp.float32),
        in_specs=[
            pl.BlockSpec(memory_space=pltpu.SMEM),
            pl.BlockSpec(memory_space=pltpu.SMEM),
            pl.BlockSpec(memory_space=pltpu.VMEM),
        ],
        out_specs=pl.BlockSpec(memory_space=pltpu.VMEM),
        scratch_shapes=[pltpu.SMEM((blocks,), jnp.int32), cube, flat]
        + [cube] * 5
        + [flat] * 6,
        compiler_params=pltpu.CompilerParams(vmem_limit_bytes=40 * 1024 * 1024),
        name="sweeps",
    )(order, owner, got)


def unpack_kernel(width, got, out_ref):
    per_tile = LANES // width
    tiles = out_ref.shape[2] // LANES
    lane = lane_of()
    for k in range(K):
        h, m = divmod(k, per_tile)
        for t in range(tiles):
            value = None
            for q in range(per_tile):
                part = rolled(got[t * per_tile + q, h], width * (q - m))
                value = part if q == 0 else jnp.where(lane < width * q, value, part)
            out_ref[k, :, LANES * t : LANES * (t + 1)] = value


def unpack(got, rows, columns):
    strips = got.shape[0]
    blocks = rows // BR
    width = columns // strips
    outs = K * width // LANES

    def kernel(*refs):
        unpack_kernel(width, *refs)

    return pl.pallas_call(
        kernel,
        grid=(blocks,),
        out_shape=jax.ShapeDtypeStruct((K, rows, columns), jnp.float32),
        in_specs=[pl.BlockSpec((strips, outs, BR, LANES), lambda b: (0, b, 0, 0))],
        out_specs=pl.BlockSpec((K, BR, columns), lambda b: (0, b, 0)),
        name="unpack",
    )(got)


def on_device(density, tracer, sea_mask, mixed_level, tile_blocks, block_owner):
    rows, columns = sea_mask.shape
    strips = lax.axis_size("gy")
    ring = lax.axis_size("gx")
    width = columns // strips
    blocks = rows // BR
    head, tail = edges(density, tracer, sea_mask, mixed_level)
    west = lax.ppermute(tail, "gx", [(i, (i + 1) % ring) for i in range(ring)])
    east = lax.ppermute(head, "gx", [((i + 1) % ring, i) for i in range(ring)])
    packed = pack(density, tracer, sea_mask, mixed_level, strips)
    packed = patch(west, east, packed, width + 2 * HALO)
    got = lax.all_to_all(packed, "gy", split_axis=0, concat_axis=0, tiled=True)
    done = sweeps(tile_blocks, block_owner, got.reshape(strips * blocks, VREGS, BR, LANES), width)
    back = lax.all_to_all(
        done.reshape(strips, -1, BR, LANES), "gy", split_axis=0, concat_axis=0, tiled=True
    )
    return unpack(back, rows, columns)


def solution(mesh):
    placed = (P(None, "gy", "gx"), P(None, "gy", "gx"), P("gy", "gx"), P("gy", "gx"), P(), P())
    return jax.shard_map(
        on_device, mesh=mesh, in_specs=placed, out_specs=P(None, "gy", "gx"), check_vma=False
    )
```

time: 616 us -> 264 us (0.43); the launches traced: 608 us -> 264 us
  waiting for transfers between devices: 336 us -> 0.01 us
  Pallas kernels: 0 us -> 194 us
  local copies, waits for them, and re-layouts: 134 us -> 1.21 us
  other arithmetic: 112 us -> 0 us
  blocking collectives: 0 us -> 67 us
  between operations: 15.3 us -> 0.02 us
  starting transfers between devices: 11.7 us -> 1.75 us
    all_gather x6 -> x0, waiting for transfers between devices: 235 us -> none  [side_by_side(): lax.all_gather(both, axis, axis=dim, tiled=True)]
    pallas_call x0 -> x5, Pallas kernels: none -> 194 us  [the longest x1 176 us: sweeps(): pl.pallas_call(kernel, out_shape=jax.ShapeDtypeStruct((blocks, outs, BR,...]
    all_to_all x1 -> x0, waiting for transfers between devices: 72.8 us -> none  [on_device(): lax.all_to_all(outgoing, 'gy', split_axis=1, concat_axis=1, tiled=True)]
    all_to_all x0 -> x2, blocking collectives: none -> 67 us  [the longest x1 47.2 us: on_device(): got = lax.all_to_all(packed, 'gy', split_axis=0, concat_axis=0, tiled=True)]
    gather x20 -> x0, local copies, waits for them, and re-layouts: 47.1 us -> none  [the longest x6 18.2 us: extend(): upper_rows = jnp.take(every_bottom, slot_above, axis=1) * has_above]
    mul x32 -> x0, other arithmetic: 32.5 us -> none  [the longest x5 10.7 us: masked_steps(): step_north = (quantity[..., 1:, :] - quantity[..., :-1, :]) * across_north]
    another operation x8 -> x0, local copies, waits for them, and re-layouts: 30.6 us -> none  [the longest x6 25.7 us: extend(): lower_rows = jnp.take(every_top, slot_below, axis=1) * has_below]
    ppermute x12 -> x2, waiting for transfers between devices: 28.1 us -> 0.01 us  [the longest x1 0.01 us: on_device(): west = lax.ppermute(tail, 'gx', [(i, (i + 1) % ring) for i in range(ring)])]
  transfers between devices with their start and end apart: 19 -> 2, of which waited for: 19 -> 0; matrix products, arithmetic and copies ran while one was open for 17% -> 0% of each run, Pallas kernels for 0% -> 3%
where the time goes in v1:
time: 264 us
  Pallas kernels  194 us (73%)
  blocking collectives  67 us (25%)
    pallas_call x1, Pallas kernels, sweeps(): pl.pallas_call(kernel, out_shape=jax.ShapeDtypeStruct((blocks, outs, BR,...  176 us
    all_to_all x1, blocking collectives, on_device(): got = lax.all_to_all(packed, 'gy', split_axis=0, concat_axis=0, tiled=True)  47.2 us
    all_to_all x1, blocking collectives, on_device(): lax.all_to_all(done.reshape(strips, -1, BR, LANES), 'gy', split_axis=0, c...  19.8 us
    pallas_call x1, Pallas kernels, pack(): pl.pallas_call(kernel, grid=(blocks,), out_shape=jax.ShapeDtypeStruct((st...  7.34 us
    pallas_call x1, Pallas kernels, unpack(): pl.pallas_call(kernel, grid=(blocks,), out_shape=jax.ShapeDtypeStruct((K,...  5.78 us
  transfers between devices with their start and end apart: 2, of which 0 were waited for; matrix products, arithmetic and copies ran while one was open for 0% of the time, Pallas kernels for 3%

profile of v1, /device:TPU:32, one launch (start us, length us, event | category | flops | bytes accessed | tf_op | source)
XLA Modules:
  0.0 263.7 jit_solution(13285755166191629134)
XLA Ops:
  0.0 2.2 edges.1
  2.2 0.0 collective-permute-start
  2.2 1.7 collective-permute-start.1
  3.9 7.3 %pack.1.refs_2_ = f32[16,48,8,128]{3,2,1,0:T(8,128)} custom-call(f32[8,64,512]{2,1,0:T(8,128)} %refs_0_.2, f32[8,64,512]{2,1,0:T(8,128)} %refs_1_.2, s32[64,512]{1,0:T(8,128)} %refs_2_.1, s32[64,512]{1,0:T(8,128)} %refs_3_.1), custom_call_target="tpu_custom_call" | custom-call | flops 20000000 | bytes 6000000 | tf_op jit(solution)/shard_map/pack/pallas_call | solution.py:134
  11.3 0.0 collective-permute-done.refs_0_
  11.3 0.0 copy-start.2
  11.3 0.0 collective-permute-done.1.refs_1_
  11.3 0.6 copy-done.2
  11.9 0.0 copy-start.3
  11.9 0.6 copy-done.3
  12.5 2.1 patch.1
  14.6 0.0 copy-start
  14.6 0.0 copy-start.1
  14.6 47.2 %all_to_all.10 = f32[16,48,8,128]{3,2,1,0:T(8,128)S(1)} all-to-all(f32[16,48,8,128]{3,2,1,0:T(8,128)} %patch.1), channel_id=1, replica_groups=mesh['gx'=8,'gy'=16] {'gy'}, dimensions={0} | all-to-all | bytes 6291456 | tf_op jit(solution)/shard_map/all_to_all | solution.py:427
  61.8 0.0 copy-done
  61.8 0.0 copy-done.1
  61.8 176.4 %sweeps.1 = f32[128,2,8,128]{3,2,1,0:T(8,128)S(1)} custom-call(s32[128]{0:T(128)S(1)} %copy-done, s32[128]{0:T(128)S(1)} %copy-done.1, f32[128,6,8,128]{3,2,1,0:T(8,128)S(1)} %bitcast.2), custom_call_target="tpu_custom_call" | custom-call | tf_op jit(solution)/shard_map/sweeps/pallas_call | solution.py:366
  238.2 19.8 %all_to_all.11.refs_0_ = f32[16,16,8,128]{3,2,1,0:T(8,128)} all-to-all(f32[16,16,8,128]{3,2,1,0:T(8,128)S(1)} %bitcast.3), channel_id=1, replica_groups=mesh['gx'=8,'gy'=16] {'gy'}, dimensions={0} | all-to-all | bytes 2097152 | tf_op jit(solution)/shard_map/all_to_all | solution.py:429
  257.9 5.8 %unpack.1 = f32[8,64,512]{2,1,0:T(8,128)} custom-call(f32[16,16,8,128]{3,2,1,0:T(8,128)} %all_to_all.11.refs_0_), custom_call_target="tpu_custom_call" | custom-call | tf_op jit(solution)/shard_map/unpack/pallas_call | solution.py:406
Async XLA Ops:
  2.2 9.1 %collective-permute-start = (f32[64,128]{1,0:T(8,128)}, f32[64,128]{1,0:T(8,128)S(1)}, u32[]{:S(2)}, u32[]{:S(2)}) collective-permute-start(f32[64,128]{1,0:T(8,128)} %get-tuple-element.7), channel_id=1, source_target_pairs={{0,16},{16,32},{32,48},{48,64},{64,80},{80,96},{96,112},{112,0},{1... | collective-permute-start | bytes 98312 | tf_op jit(solution)/shard_map/ppermute | solution.py:423
  2.2 9.1 %collective-permute-start.1 = (f32[64,128]{1,0:T(8,128)}, f32[64,128]{1,0:T(8,128)S(1)}, u32[]{:S(2)}, u32[]{:S(2)}) collective-permute-start(f32[64,128]{1,0:T(8,128)} %get-tuple-element.8), channel_id=1, source_target_pairs={{16,0},{32,16},{48,32},{64,48},{80,64},{96,80},{112,96},{0,112},{1... | collective-permute-start | bytes 98312 | tf_op jit(solution)/shard_map/ppermute | solution.py:424
  11.3 0.6 copy-start.2
  11.9 0.6 copy-start.3
  14.6 47.2 %copy-start = (s32[128]{0:T(128)S(1)}, s32[128]{0:T(128)}, u32[]{:S(2)}) copy-start(s32[128]{0:T(128)} %refs_0_.3) | copy-start | bytes 1540
  14.6 47.2 %copy-start.1 = (s32[128]{0:T(128)S(1)}, s32[128]{0:T(128)}, u32[]{:S(2)}) copy-start(s32[128]{0:T(128)} %refs_1_.3) | copy-start | bytes 1540

commit v2 on v1

--- a/solution.py
+++ b/solution.py
@@ -11,8 +11,13 @@
 HALO = ITERS + 1
 LANES = 128
 SLOTS = 3
-GROUPS = 3
 VREGS = 6
+UNIT = 4
+GATHER = 4
+PHYSICS = 2
+FACES = 4
+SWEEP = 4
+LAST = 4
 
 TIME_STEP = 0.2
 STRATIFICATION = 1.0
@@ -181,182 +186,183 @@
 
 
 def sweep_kernel(
-    width, blocks, order, owner, got, out_ref, slot_of, rho, sea, ta, tb, cp, cq, cr, kap, ce, cw, cn, me, mw
+    width, blocks, order, owner, got, out_ref, slot_of, rho, ta, tb, cp, cq, cr, sea, mix, kap, me, mw, mn, ms, ce, cw, cn, cs
 ):
     piece = width + 2 * HALO
+    depth = (sea.shape[0] - 2 * BR) // BR
     lane = lane_of()
     first = lane < piece
     second = lane < 2 * piece
-    slot = jnp.where(first, 0, jnp.where(second, 1, 2))
-    zeros = jnp.zeros((BR, LANES), jnp.float32)
 
     def invert(s, carry):
         slot_of[order[s]] = s
         return carry
 
     lax.fori_loop(0, blocks, invert, 0)
-
-    for edge in (0, BR * (blocks + 1)):
-        for g in range(GROUPS):
-            rho[g, pl.ds(edge, BR), :] = zeros
-            ta[g, pl.ds(edge, BR), :] = zeros
-            tb[g, pl.ds(edge, BR), :] = zeros
-        sea[pl.ds(edge, BR), :] = zeros
-        kap[pl.ds(edge, BR), :] = zeros
-        cn[pl.ds(edge, BR), :] = zeros
-
-    def spread(x):
-        return jnp.where(first, rolled(x, -2 * piece), jnp.where(second, rolled(x, -piece), x))
-
-    def loop(body, step=1):
+    for b in range(blocks, SLOTS * depth):
+        slot_of[b] = slot_of[0]
+
+    def loop(body, count, chunk):
         def some(i, carry):
-            for u in range(step):
-                body(i * step + u)
+            body(i)
             return carry
 
-        lax.fori_loop(0, blocks // step, some, 0)
-
-    def rows(b, off=0):
+        lax.fori_loop(0, count // chunk, some, 0)
+
+    def rows(c, off=0, chunk=1):
+        start = BR + BR * chunk * c
         if off == 0:
-            return pl.ds(pl.multiple_of(BR * (b + 1), BR), BR)
-        return pl.ds(BR * (b + 1) + off, BR)
-
-    def gather(b):
-        s = slot_of[b]
-        t = owner[s]
-        for g in range(GROUPS):
-            rho[g, rows(b), :] = got[s, g]
-            ta[g, rows(b), :] = got[t, GROUPS + g]
-        sea[rows(b), :] = spread(got[s, 2])
-
-    loop(gather, 2)
-
-    def deltas(f):
-        f0, f1, f2 = f
-        f2 = jnp.where(second, f2, f1)
-        above0 = jnp.where(first, f0, rolled(f2, piece))
-        return (f1 - above0, f2 - f0, rolled(f0, -piece) - f1)
-
-    def physics(b):
-        s = slot_of[b]
-        mixed = spread(got[s, 5])
-        here = sea[rows(b), :]
-        north = sea[rows(b, 1), :] * here
-        south = sea[rows(b, -1), :] * here
+            return pl.ds(pl.multiple_of(start, BR), BR * chunk)
+        return pl.ds(start + off, BR * chunk)
+
+    def close(ref):
+        top = jnp.where(first, 0.0, rolled(ref[pl.ds(BR * depth, BR), :], piece))
+        bottom = jnp.where(second, rolled(ref[pl.ds(BR, BR), :], -piece), 0.0)
+        ref[pl.ds(0, BR), :] = top
+        ref[pl.ds(BR * (depth + 1), BR), :] = bottom
+
+    def gather(c):
+        for u in range(GATHER):
+            i = c * GATHER + u
+            slots = [slot_of[i + depth * m] for m in range(SLOTS)]
+            owners = [owner[s] for s in slots]
+            real = jnp.where(i + depth * (SLOTS - 1) < blocks, 1.0, 0.0)
+
+            def plane(v, n, where):
+                parts = [rolled(got[where[m], v], piece * (m - n)) for m in range(SLOTS)]
+                return jnp.where(first, parts[0], jnp.where(second, parts[1], parts[2] * real))
+
+            at = rows(i)
+            for k in range(K):
+                rho[k, at, :] = plane(k % 3, k // 3, slots)
+                ta[k, at, :] = plane(3 + k % 3, k // 3, owners)
+            sea[at, :] = plane(2, 2, slots)
+            mix[at, :] = plane(5, 2, slots)
+
+    loop(gather, depth, GATHER)
+    for k in range(K):
+        close(rho.at[k])
+        close(ta.at[k])
+    close(sea)
+
+    def physics(c):
+        at, up, down = (rows(c, off, PHYSICS) for off in (0, 1, -1))
+        mixed = mix[at, :]
+        here = sea[at, :]
         east = rolled(here, -1) * here
-        west = rolled(east, 1)
-        me[rows(b), :] = east
-        mw[rows(b), :] = west
-        f = [rho[g, rows(b), :] for g in range(GROUPS)]
-        down = deltas(f)
+        west = rolled(here, 1) * here
+        north = sea[up, :] * here
+        south = sea[down, :] * here
+        me[at, :] = east
+        mw[at, :] = west
+        mn[at, :] = north
+        ms[at, :] = south
         per_mixed = 1.0 / (mixed + 1.0)
-        total = zeros
+        f = [rho[k, at, :] for k in range(K)]
+        total = jnp.zeros_like(here)
         kept = []
-        for g in range(GROUPS):
-            level = (slot * 3 + g).astype(jnp.float32)
-            step = rolled(f[g], -1) - f[g]
-            sum_e = east * step + west * rolled(step, 1)
-            sum_n = north * (rho[g, rows(b, 1), :] - f[g]) + south * (f[g] - rho[g, rows(b, -1), :])
-            rising = jnp.where((level == 0.0) | (level == K - 1.0), 0.5 * STRATIFICATION, STRATIFICATION)
-            denominator = jnp.maximum(0.5 * down[g] + rising, DENSITY_FLOOR)
+        for k in range(K):
+            sum_e = east * (rolled(f[k], -1) - f[k]) + west * (f[k] - rolled(f[k], 1))
+            sum_n = north * (rho[k, up, :] - f[k]) + south * (f[k] - rho[k, down, :])
+            above, under = max(k - 1, 0), min(k + 1, K - 1)
+            rising = 0.5 * STRATIFICATION * (under - above)
+            denominator = jnp.maximum(0.5 * (f[under] - f[above]) + rising, DENSITY_FLOOR)
             scale = -0.5 / denominator
             se = sum_e * scale
             sn = sum_n * scale
             squared = se * se + sn * sn
             taper = 0.5 + 0.5 * jnp.tanh((SLOPE_LIMIT - squared) * (1.0 / TAPER_WIDTH))
-            factor = taper * jnp.minimum(1.0, (level + 1.0) * per_mixed) * here
+            factor = taper * jnp.minimum(1.0, (k + 1.0) * per_mixed) * here
             se = se * factor
             sn = sn * factor
             squared = se * se + sn * sn
-            below = (level >= mixed) & (level < K)
-            total += jnp.where(below, jnp.sqrt(denominator * (squared + KERNEL_OFFSET)), 0.0)
-            kept.append((se, sn, squared))
-        total = total + rolled(total, -piece) + rolled(total, -2 * piece)
-        total = jnp.where(first, total, jnp.where(second, rolled(total, piece), rolled(total, 2 * piece)))
+            root = jnp.sqrt(denominator * (squared + KERNEL_OFFSET))
+            total += jnp.where(mixed <= float(k), root, 0.0)
+            cp[k, at, :] = se
+            cq[k, at, :] = sn
+            kept.append(squared)
         kappa = here * (BASE_DIFFUSIVITY + VISBECK_ALPHA * total / (K - mixed))
-        kap[rows(b), :] = kappa
+        kap[at, :] = kappa
         weight = (0.5 * TIME_STEP) * kappa
-        for g in range(GROUPS):
-            se, sn, squared = kept[g]
-            w = jnp.where(second, weight, 0.0) if g == 2 else weight
-            cp[g, rows(b), :] = w * se
-            cq[g, rows(b), :] = w * sn
-            cr[g, rows(b), :] = (0.5 * w) * squared
-
-    loop(physics)
-
-    def faces(b):
-        kappa = kap[rows(b), :]
-        here = sea[rows(b), :]
-        east = (0.5 * TIME_STEP) * (kappa + rolled(kappa, -1)) * me[rows(b), :]
-        ce[rows(b), :] = east
-        cw[rows(b), :] = rolled(east, 1)
-        cn[rows(b), :] = (0.5 * TIME_STEP) * (kappa + kap[rows(b, 1), :]) * (here * sea[rows(b, 1), :])
-
-    loop(faces, 2)
-
-    def advance(b, source):
-        here = sea[rows(b), :]
-        north = sea[rows(b, 1), :] * here
-        south = sea[rows(b, -1), :] * here
-        east = me[rows(b), :]
-        west = mw[rows(b), :]
-        face_e = ce[rows(b), :]
-        face_w = cw[rows(b), :]
-        face_n = cn[rows(b), :]
-        face_s = cn[rows(b, -1), :]
-        f = [source[g, rows(b), :] for g in range(GROUPS)]
-        down = deltas(f)
+        for k in range(K):
+            cp[k, at, :] = weight * cp[k, at, :]
+            cq[k, at, :] = weight * cq[k, at, :]
+            cr[k, at, :] = (0.5 * weight) * kept[k]
+
+    loop(physics, depth, PHYSICS)
+    close(kap)
+
+    def faces(c):
+        at, up, down = (rows(c, off, FACES) for off in (0, 1, -1))
+        kappa = (0.5 * TIME_STEP) * kap[at, :]
+        ce[at, :] = (kappa + rolled(kappa, -1)) * me[at, :]
+        cw[at, :] = (kappa + rolled(kappa, 1)) * mw[at, :]
+        cn[at, :] = (kappa + (0.5 * TIME_STEP) * kap[up, :]) * mn[at, :]
+        cs[at, :] = (kappa + (0.5 * TIME_STEP) * kap[down, :]) * ms[at, :]
+
+    loop(faces, depth, FACES)
+
+    def advance(c, source, chunk):
+        at, up, down = (rows(c, off, chunk) for off in (0, 1, -1))
+        mask_e, mask_w, mask_n, mask_s = (ref[at, :] for ref in (me, mw, mn, ms))
+        face_e, face_w, face_n, face_s = (ref[at, :] for ref in (ce, cw, cn, cs))
+        f = [source[k, at, :] for k in range(K)]
         flux, result = [], []
-        for g in range(GROUPS):
-            step_e = rolled(f[g], -1) - f[g]
-            step_w = rolled(step_e, 1)
-            step_n = source[g, rows(b, 1), :] - f[g]
-            step_s = f[g] - source[g, rows(b, -1), :]
-            sum_e = east * step_e + west * step_w
-            sum_n = north * step_n + south * step_s
+        for k in range(K):
+            step_e = rolled(f[k], -1) - f[k]
+            step_w = f[k] - rolled(f[k], 1)
+            step_n = source[k, up, :] - f[k]
+            step_s = f[k] - source[k, down, :]
+            sum_e = mask_e * step_e + mask_w * step_w
+            sum_n = mask_n * step_n + mask_s * step_s
             lateral = (face_e * step_e - face_w * step_w) + (face_n * step_n - face_s * step_s)
-            flux.append(
-                cp[g, rows(b), :] * sum_e + cq[g, rows(b), :] * sum_n + cr[g, rows(b), :] * down[g]
-            )
-            result.append(f[g] + lateral)
-        result[0] += flux[1] - rolled(flux[2], piece)
-        result[1] += flux[2] - flux[0]
-        result[2] += rolled(flux[0], -piece) - flux[1]
+            drop = f[min(k + 1, K - 1)] - f[max(k - 1, 0)]
+            flux.append(cp[k, at, :] * sum_e + cq[k, at, :] * sum_n + cr[k, at, :] * drop)
+            result.append(f[k] + lateral)
+        for k in range(K):
+            if k + 1 < K:
+                result[k] += flux[k + 1]
+            if k > 0:
+                result[k] -= flux[k - 1]
         return result
 
     def sweep(source, target):
-        def body(b):
-            result = advance(b, source)
-            for g in range(GROUPS):
-                target[g, rows(b), :] = result[g]
-
-        loop(body)
-
-    sweep(ta, tb)
-    sweep(tb, ta)
-    sweep(ta, tb)
-
+        def body(c):
+            result = advance(c, source, SWEEP)
+            for k in range(K):
+                target[k, rows(c, 0, SWEEP), :] = result[k]
+
+        loop(body, depth, SWEEP)
+        for k in range(K):
+            close(target.at[k])
+
+    for n in range(ITERS - 1):
+        sweep(*((ta, tb) if n % 2 == 0 else (tb, ta)))
+    source = ta if (ITERS - 1) % 2 == 0 else tb
     per_out = LANES // width
-
-    def last(b):
-        result = advance(b, tb)
-        t = owner[slot_of[b]]
-        for h in range(K // per_out):
-            value = None
-            for m in range(per_out):
-                k = h * per_out + m
-                part = rolled(result[k % 3], width * m - (piece * (k // 3) + HALO))
-                value = part if m == 0 else jnp.where(lane < width * m, value, part)
-            out_ref[t, h] = value
-
-    loop(last)
+    wide = lane_of((BR * LAST, LANES))
+
+    def last(back):
+        c = depth // LAST - 1 - back
+        result = advance(c, source, LAST)
+        for g in reversed(range(SLOTS)):
+            for h in range(K // per_out):
+                value = None
+                for m in range(per_out):
+                    part = rolled(result[h * per_out + m], width * m - (piece * g + HALO))
+                    value = part if m == 0 else jnp.where(wide < width * m, value, part)
+                for u in range(LAST):
+                    t = owner[slot_of[c * LAST + u + depth * g]]
+                    out_ref[t, h] = value[BR * u : BR * (u + 1), :]
+
+    loop(last, depth, LAST)
 
 
 def sweeps(order, owner, got, width):
     blocks = got.shape[0]
-    padded = BR * (blocks + 2)
-    cube = pltpu.VMEM((GROUPS, padded, LANES), jnp.float32)
+    depth = -(-blocks // (SLOTS * UNIT)) * UNIT
+    padded = BR * (depth + 2)
+    cube = pltpu.VMEM((K, padded, LANES), jnp.float32)
     flat = pltpu.VMEM((padded, LANES), jnp.float32)
     outs = K * width // LANES
 
@@ -372,9 +378,7 @@
             pl.BlockSpec(memory_space=pltpu.VMEM),
         ],
         out_specs=pl.BlockSpec(memory_space=pltpu.VMEM),
-        scratch_shapes=[pltpu.SMEM((blocks,), jnp.int32), cube, flat]
-        + [cube] * 5
-        + [flat] * 6,
+        scratch_shapes=[pltpu.SMEM((SLOTS * depth,), jnp.int32)] + [cube] * 6 + [flat] * 11,
         compiler_params=pltpu.CompilerParams(vmem_limit_bytes=40 * 1024 * 1024),
         name="sweeps",
     )(order, owner, got)

time: 264 us -> 106 us (0.40)
  Pallas kernels: 194 us -> 35.1 us
    pallas_call x1, Pallas kernels: 176 us -> 17.7 us  [sweeps(): pl.pallas_call(kernel, out_shape=jax.ShapeDtypeStruct((blocks, outs, BR,...]
  transfers between devices with their start and end apart: 2 -> 2, of which waited for: 0 -> 0; matrix products, arithmetic and copies ran while one was open for 0% -> 0% of each run, Pallas kernels for 3% -> 7%
where the time goes in v2:
time: 106 us; the launch traced here: 105 us
  blocking collectives  67 us (63%)
  Pallas kernels  35.1 us (33%)
  starting transfers between devices  1.75 us (2%)
  local copies, waits for them, and re-layouts  1.21 us (1%)
    all_to_all x1, blocking collectives, on_device(): got = lax.all_to_all(packed, 'gy', split_axis=0, concat_axis=0, tiled=True)  47.2 us
    all_to_all x1, blocking collectives, on_device(): lax.all_to_all(done.reshape(strips, -1, BR, LANES), 'gy', split_axis=0, c...  19.8 us
    pallas_call x1, Pallas kernels, sweeps(): pl.pallas_call(kernel, out_shape=jax.ShapeDtypeStruct((blocks, outs, BR,...  17.7 us
    pallas_call x1, Pallas kernels, pack(): pl.pallas_call(kernel, grid=(blocks,), out_shape=jax.ShapeDtypeStruct((st...  7.34 us
    pallas_call x1, Pallas kernels, unpack(): pl.pallas_call(kernel, grid=(blocks,), out_shape=jax.ShapeDtypeStruct((K,...  5.78 us
    pallas_call x1, Pallas kernels, edges(): pl.pallas_call(edges_kernel, grid=(1,), out_shape=(out, out), out_specs=(...  2.19 us
  transfers between devices with their start and end apart: 2, of which 0 were waited for; matrix products, arithmetic and copies ran while one was open for 0% of the time, Pallas kernels for 7%

profile of v2, /device:TPU:32, one launch (start us, length us, event | category | flops | bytes accessed | tf_op | source)
XLA Modules:
  0.0 105.1 jit_solution(667204852295875894)
XLA Ops:
  0.0 2.2 %edges.1 = (f32[64,128]{1,0:T(8,128)}, f32[64,128]{1,0:T(8,128)}) custom-call(f32[8,64,512]{2,1,0:T(8,128)} %refs_0_.2, f32[8,64,512]{2,1,0:T(8,128)} %refs_0_.2, f32[8,64,512]{2,1,0:T(8,128)} %refs_1_.2, f32[8,64,512]{2,1,0:T(8,128)} %refs_1_.2, s32[64,512]{1,0:T(8,128)} %refs_2_.1, s32[64,512]{1,0:T(8,128)} %refs_2_.1, s32[64,512]{1,0:T(8,128)} %refs_3_.1, ...), custom_call_target="tpu_custom_call" | custom-call | tf_op jit(solution)/shard_map/edges/pallas_call | solution.py:77
  2.2 0.0 collective-permute-start
  2.2 1.7 %collective-permute-start.1 = (f32[64,128]{1,0:T(8,128)}, f32[64,128]{1,0:T(8,128)S(1)}, u32[]{:S(2)}, u32[]{:S(2)}) collective-permute-start(f32[64,128]{1,0:T(8,128)} %get-tuple-element.8), channel_id=1, source_target_pairs={{16,0},{32,16},{48,32},{64,48},{80,64},{96,80},{112,96},{0,112},{1... | collective-permute-start | bytes 98312 | tf_op jit(solution)/shard_map/ppermute | solution.py:428
  3.9 7.3 %pack.1.refs_2_ = f32[16,48,8,128]{3,2,1,0:T(8,128)} custom-call(f32[8,64,512]{2,1,0:T(8,128)} %refs_0_.2, f32[8,64,512]{2,1,0:T(8,128)} %refs_1_.2, s32[64,512]{1,0:T(8,128)} %refs_2_.1, s32[64,512]{1,0:T(8,128)} %refs_3_.1), custom_call_target="tpu_custom_call" | custom-call | flops 20000000 | bytes 6000000 | tf_op jit(solution)/shard_map/pack/pallas_call | solution.py:139
  11.3 0.0 collective-permute-done.refs_0_
  11.3 0.0 copy-start.2
  11.3 0.0 collective-permute-done.1.refs_1_
  11.3 0.6 copy-done.2
  11.9 0.0 copy-start.3
  11.9 0.6 copy-done.3
  12.5 2.1 %patch.1 = f32[16,48,8,128]{3,2,1,0:T(8,128)} custom-call(f32[64,128]{1,0:T(8,128)} %copy-done.2, f32[64,128]{1,0:T(8,128)} %copy-done.3, f32[16,48,8,128]{3,2,1,0:T(8,128)} %pack.1.refs_2_), custom_call_target="tpu_custom_call", output_to_operand_aliasing={{}: (2, {})} | custom-call | tf_op jit(solution)/shard_map/patch/pallas_call | solution.py:177
  14.6 0.0 copy-start
  14.6 0.0 copy-start.1
  14.6 47.2 %all_to_all.10 = f32[16,48,8,128]{3,2,1,0:T(8,128)S(1)} all-to-all(f32[16,48,8,128]{3,2,1,0:T(8,128)} %patch.1), channel_id=1, replica_groups=mesh['gx'=8,'gy'=16] {'gy'}, dimensions={0} | all-to-all | bytes 6291456 | tf_op jit(solution)/shard_map/all_to_all | solution.py:431
  61.8 0.0 copy-done
  61.8 0.0 copy-done.1
  61.8 17.7 %sweeps.1 = f32[128,2,8,128]{3,2,1,0:T(8,128)S(1)} custom-call(s32[128]{0:T(128)S(1)} %copy-done, s32[128]{0:T(128)S(1)} %copy-done.1, f32[128,6,8,128]{3,2,1,0:T(8,128)S(1)} %bitcast.2), custom_call_target="tpu_custom_call" | custom-call | tf_op jit(solution)/shard_map/sweeps/pallas_call | solution.py:372
  79.5 19.8 %all_to_all.11.refs_0_ = f32[16,16,8,128]{3,2,1,0:T(8,128)} all-to-all(f32[16,16,8,128]{3,2,1,0:T(8,128)S(1)} %bitcast.3), channel_id=1, replica_groups=mesh['gx'=8,'gy'=16] {'gy'}, dimensions={0} | all-to-all | bytes 2097152 | tf_op jit(solution)/shard_map/all_to_all | solution.py:433
  99.3 5.8 %unpack.1 = f32[8,64,512]{2,1,0:T(8,128)} custom-call(f32[16,16,8,128]{3,2,1,0:T(8,128)} %all_to_all.11.refs_0_), custom_call_target="tpu_custom_call" | custom-call | tf_op jit(solution)/shard_map/unpack/pallas_call | solution.py:410
Async XLA Ops:
  2.2 9.1 %collective-permute-start = (f32[64,128]{1,0:T(8,128)}, f32[64,128]{1,0:T(8,128)S(1)}, u32[]{:S(2)}, u32[]{:S(2)}) collective-permute-start(f32[64,128]{1,0:T(8,128)} %get-tuple-element.7), channel_id=1, source_target_pairs={{0,16},{16,32},{32,48},{48,64},{64,80},{80,96},{96,112},{112,0},{1... | collective-permute-start | bytes 98312 | tf_op jit(solution)/shard_map/ppermute | solution.py:427
  2.2 9.1 %collective-permute-start.1 = (f32[64,128]{1,0:T(8,128)}, f32[64,128]{1,0:T(8,128)S(1)}, u32[]{:S(2)}, u32[]{:S(2)}) collective-permute-start(f32[64,128]{1,0:T(8,128)} %get-tuple-element.8), channel_id=1, source_target_pairs={{16,0},{32,16},{48,32},{64,48},{80,64},{96,80},{112,96},{0,112},{1... | collective-permute-start | bytes 98312 | tf_op jit(solution)/shard_map/ppermute | solution.py:428
  11.3 0.6 copy-start.2
  11.9 0.6 copy-start.3
  14.6 47.2 %copy-start = (s32[128]{0:T(128)S(1)}, s32[128]{0:T(128)}, u32[]{:S(2)}) copy-start(s32[128]{0:T(128)} %refs_0_.3) | copy-start | bytes 1540
  14.6 47.2 %copy-start.1 = (s32[128]{0:T(128)S(1)}, s32[128]{0:T(128)}, u32[]{:S(2)}) copy-start(s32[128]{0:T(128)} %refs_1_.3) | copy-start | bytes 1540

commit v3 on v2

--- a/solution.py
+++ b/solution.py
@@ -12,9 +12,12 @@
 LANES = 128
 SLOTS = 3
 VREGS = 6
+PACK = 2
+UNPACK = 2
+SMALL = 12 * 1024 * 1024
 UNIT = 4
-GATHER = 4
-PHYSICS = 2
+GATHER = 11
+PHYSICS = 4
 FACES = 4
 SWEEP = 4
 LAST = 4
@@ -79,6 +82,7 @@
         grid=(1,),
         out_shape=(out, out),
         out_specs=(rim, rim),
+        compiler_params=pltpu.CompilerParams(vmem_limit_bytes=SMALL),
         in_specs=[cube(0), cube(last), cube(0), cube(last), flat(0), flat(last), flat(0), flat(last)],
         name="edges",
     )(density, density, tracer, tracer, mask, mask, mixed, mixed)
@@ -88,60 +92,65 @@
     piece = width + 2 * HALO
     per_tile = LANES // width
     tiles = mask.shape[1] // LANES
+    count = mask.shape[0] // BR
     lane = lane_of()
 
-    def columns(p):
+    def columns(p, row):
         for t in range(tiles):
             at = slice(LANES * t, LANES * (t + 1))
             if p < K:
-                yield density[p, :, at]
+                yield density[p, row, at]
             elif p < 2 * K:
-                yield tracer[p - K, :, at]
+                yield tracer[p - K, row, at]
             else:
-                yield (mask if p == 2 * K else mixed)[:, at].astype(jnp.float32)
-
-    for v in range(VREGS):
-        whole, seam = [], []
-        for m in range(SLOTS):
-            own = list(columns(plane_at(v, m)))
-            whole.append(own)
-            seam.append(
-                [own[0]]
-                + [jnp.where(lane < LANES // 2, own[t], own[t - 1]) for t in range(1, tiles)]
-                + [own[-1]]
-            )
-        for j in range(tiles * per_tile):
-            t, q = divmod(j, per_tile)
-            parts = []
+                yield (mask if p == 2 * K else mixed)[row, at].astype(jnp.float32)
+
+    for u in range(count):
+        block = pl.program_id(0) * count + u
+        for v in range(VREGS):
+            whole, seam = [], []
             for m in range(SLOTS):
-                if q == 0:
-                    source = seam[m][t]
-                elif q == per_tile - 1:
-                    source = seam[m][t + 1]
-                else:
-                    source = whole[m][t]
-                parts.append(rolled(source, piece * m - (width * q - HALO)))
-            out_ref[j, v] = jnp.where(
-                lane < piece, parts[0], jnp.where(lane < 2 * piece, parts[1], parts[2])
-            )
+                own = list(columns(plane_at(v, m), slice(BR * u, BR * (u + 1))))
+                whole.append(own)
+                seam.append(
+                    [own[0]]
+                    + [jnp.where(lane < LANES // 2, own[t], own[t - 1]) for t in range(1, tiles)]
+                    + [own[-1]]
+                )
+            for j in range(tiles * per_tile):
+                t, q = divmod(j, per_tile)
+                parts = []
+                for m in range(SLOTS):
+                    if q == 0:
+                        source = seam[m][t]
+                    elif q == per_tile - 1:
+                        source = seam[m][t + 1]
+                    else:
+                        source = whole[m][t]
+                    parts.append(rolled(source, piece * m - (width * q - HALO)))
+                out_ref[j, block * VREGS + v] = jnp.where(
+                    lane < piece, parts[0], jnp.where(lane < 2 * piece, parts[1], parts[2])
+                )
 
 
 def pack(density, tracer, mask, mixed, strips):
     rows, columns = mask.shape
     blocks = rows // BR
     width = columns // strips
-    cube = pl.BlockSpec((K, BR, columns), lambda b: (0, b, 0))
-    flat = pl.BlockSpec((BR, columns), lambda b: (b, 0))
+    tall = rows // PACK
+    cube = pl.BlockSpec((K, tall, columns), lambda b: (0, b, 0))
+    flat = pl.BlockSpec((tall, columns), lambda b: (b, 0))
 
     def kernel(*refs):
         pack_kernel(width, *refs)
 
     return pl.pallas_call(
         kernel,
-        grid=(blocks,),
+        grid=(PACK,),
         out_shape=jax.ShapeDtypeStruct((strips, blocks * VREGS, BR, LANES), jnp.float32),
         in_specs=[cube, cube, flat, flat],
-        out_specs=pl.BlockSpec((strips, VREGS, BR, LANES), lambda b: (0, b, 0, 0)),
+        out_specs=pl.BlockSpec(memory_space=pltpu.VMEM),
+        compiler_params=pltpu.CompilerParams(vmem_limit_bytes=SMALL),
         cost_estimate=pl.CostEstimate(flops=20000000, bytes_accessed=6000000, transcendentals=0),
         name="pack",
     )(density, tracer, mask, mixed)
@@ -149,38 +158,37 @@
 
 def patch_kernel(piece, west, east, packed, out_ref):
     lane = lane_of()
+    strips = packed.shape[0]
     blocks = west.shape[0] // BR
 
-    def fill(edge, start):
-        for b in range(blocks):
-            rim = edge[BR * b : BR * (b + 1), :]
-            for v in range(VREGS):
-                value = packed[0, b * VREGS + v]
-                for m in range(SLOTS):
-                    at = piece * m + start
-                    here = (lane >= at) & (lane < at + HALO)
-                    value = jnp.where(here, rolled(rim, at - HALO * plane_at(v, m)), value)
-                out_ref[0, b * VREGS + v] = value
-
-    pl.when(pl.program_id(0) == 0)(lambda: fill(west, 0))
-    pl.when(pl.program_id(0) == 1)(lambda: fill(east, piece - HALO))
+    def fill(b, strip, edge, start):
+        rim = edge[pl.ds(pl.multiple_of(BR * b, BR), BR), :]
+        for v in range(VREGS):
+            value = packed[strip, b * VREGS + v]
+            for m in range(SLOTS):
+                at = piece * m + start
+                here = (lane >= at) & (lane < at + HALO)
+                value = jnp.where(here, rolled(rim, at - HALO * plane_at(v, m)), value)
+            out_ref[strip, b * VREGS + v] = value
+
+    for b in range(blocks):
+        fill(b, 0, west, 0)
+        fill(b, strips - 1, east, piece - HALO)
 
 
 def patch(west, east, packed, piece):
-    strips, count = packed.shape[:2]
-    rim = pl.BlockSpec(west.shape, lambda i: (0, 0))
-    ends = pl.BlockSpec((1, count, BR, LANES), lambda i: (i * (strips - 1), 0, 0, 0))
+    whole = pl.BlockSpec(memory_space=pltpu.VMEM)
 
     def kernel(*refs):
         patch_kernel(piece, *refs)
 
     return pl.pallas_call(
         kernel,
-        grid=(2,),
         out_shape=jax.ShapeDtypeStruct(packed.shape, jnp.float32),
-        in_specs=[rim, rim, ends],
-        out_specs=ends,
+        in_specs=[whole, whole, whole],
+        out_specs=whole,
         input_output_aliases={2: 0},
+        compiler_params=pltpu.CompilerParams(vmem_limit_bytes=SMALL),
         name="patch",
     )(west, east, packed)
 
@@ -198,7 +206,7 @@
         slot_of[order[s]] = s
         return carry
 
-    lax.fori_loop(0, blocks, invert, 0)
+    lax.fori_loop(0, blocks, invert, 0, unroll=8)
     for b in range(blocks, SLOTS * depth):
         slot_of[b] = slot_of[0]
 
@@ -387,32 +395,36 @@
 def unpack_kernel(width, got, out_ref):
     per_tile = LANES // width
     tiles = out_ref.shape[2] // LANES
+    count = out_ref.shape[1] // BR
+    outs = K // per_tile
     lane = lane_of()
-    for k in range(K):
-        h, m = divmod(k, per_tile)
-        for t in range(tiles):
-            value = None
-            for q in range(per_tile):
-                part = rolled(got[t * per_tile + q, h], width * (q - m))
-                value = part if q == 0 else jnp.where(lane < width * q, value, part)
-            out_ref[k, :, LANES * t : LANES * (t + 1)] = value
+    for u in range(count):
+        block = pl.program_id(0) * count + u
+        for k in range(K):
+            h, m = divmod(k, per_tile)
+            for t in range(tiles):
+                value = None
+                for q in range(per_tile):
+                    part = rolled(got[t * per_tile + q, block * outs + h], width * (q - m))
+                    value = part if q == 0 else jnp.where(lane < width * q, value, part)
+                out_ref[k, BR * u : BR * (u + 1), LANES * t : LANES * (t + 1)] = value
 
 
 def unpack(got, rows, columns):
     strips = got.shape[0]
     blocks = rows // BR
     width = columns // strips
-    outs = K * width // LANES
 
     def kernel(*refs):
         unpack_kernel(width, *refs)
 
     return pl.pallas_call(
         kernel,
-        grid=(blocks,),
+        grid=(UNPACK,),
         out_shape=jax.ShapeDtypeStruct((K, rows, columns), jnp.float32),
-        in_specs=[pl.BlockSpec((strips, outs, BR, LANES), lambda b: (0, b, 0, 0))],
-        out_specs=pl.BlockSpec((K, BR, columns), lambda b: (0, b, 0)),
+        in_specs=[pl.BlockSpec(memory_space=pltpu.VMEM)],
+        out_specs=pl.BlockSpec((K, rows // UNPACK, columns), lambda b: (0, b, 0)),
+        compiler_params=pltpu.CompilerParams(vmem_limit_bytes=SMALL),
         name="unpack",
     )(got)
 

time: 106 us -> 94.7 us (0.89)
  Pallas kernels: 35.1 us -> 20.8 us
  local copies, waits for them, and re-layouts: 1.21 us -> 4.27 us
    pallas_call x3, Pallas kernels: 15.2 us -> 4.9 us  [the longest x1 2.74 us: pack(): pl.pallas_call(kernel, grid=(PACK,), out_shape=jax.ShapeDtypeStruct((stri...]
    unnamed x8 -> x12, local copies, waits for them, and re-layouts: 1.21 us -> 4.27 us
    pallas_call x1, Pallas kernels: 17.7 us -> 15.5 us  [sweeps(): pl.pallas_call(kernel, out_shape=jax.ShapeDtypeStruct((blocks, outs, BR,...]
    pallas_call x1, Pallas kernels: 2.19 us -> 0.36 us  [edges(): pl.pallas_call(edges_kernel, grid=(1,), out_shape=(out, out), out_specs=(...]
  transfers between devices with their start and end apart: 2 -> 2, of which waited for: 0 -> 0; matrix products, arithmetic and copies ran while one was open for 0% -> 0% of each run, Pallas kernels for 7% -> 3%
where the time goes in v3:
time: 94.7 us; the launch traced here: 94.4 us
  blocking collectives  67.5 us (71%)
  Pallas kernels  20.8 us (22%)
  local copies, waits for them, and re-layouts  4.27 us (5%)
  starting transfers between devices  1.75 us (2%)
    all_to_all x1, blocking collectives, on_device(): got = lax.all_to_all(packed, 'gy', split_axis=0, concat_axis=0, tiled=True)  47.4 us
    all_to_all x1, blocking collectives, on_device(): lax.all_to_all(done.reshape(strips, -1, BR, LANES), 'gy', split_axis=0, c...  20.1 us
    pallas_call x1, Pallas kernels, sweeps(): pl.pallas_call(kernel, out_shape=jax.ShapeDtypeStruct((blocks, outs, BR,...  15.5 us
    unnamed x12, local copies, waits for them, and re-layouts  4.27 us
    pallas_call x1, Pallas kernels, pack(): pl.pallas_call(kernel, grid=(PACK,), out_shape=jax.ShapeDtypeStruct((stri...  2.74 us
  transfers between devices with their start and end apart: 2, of which 0 were waited for; matrix products, arithmetic and copies ran while one was open for 0% of the time, Pallas kernels for 3%

profile of v3, /device:TPU:32, one launch (start us, length us, event | category | flops | bytes accessed | tf_op | source)
XLA Modules:
  0.0 94.4 jit_solution(501207515233708910)
XLA Ops:
  0.0 0.0 copy-start
  0.0 1.2 %copy-done = f32[8,64,512]{2,1,0:T(8,128)S(1)} copy-done((f32[8,64,512]{2,1,0:T(8,128)S(1)}, f32[8,64,512]{2,1,0:T(8,128)}, u32[]{:S(2)}) %copy-start) | copy-done | bytes 1048600
  1.2 0.0 copy-start.1
  1.2 1.2 %copy-done.1 = f32[8,64,512]{2,1,0:T(8,128)S(1)} copy-done((f32[8,64,512]{2,1,0:T(8,128)S(1)}, f32[8,64,512]{2,1,0:T(8,128)}, u32[]{:S(2)}) %copy-start.1) | copy-done | bytes 1048600
  2.5 0.0 copy-start.2
  2.5 0.9 copy-done.2
  3.4 0.0 copy-start.3
  3.4 0.9 copy-done.3
  4.3 0.4 edges.1
  4.6 0.0 collective-permute-start
  4.7 1.7 %collective-permute-start.1 = (f32[64,128]{1,0:T(8,128)S(1)}, f32[64,128]{1,0:T(8,128)S(1)}, u32[]{:S(2)}, u32[]{:S(2)}) collective-permute-start(f32[64,128]{1,0:T(8,128)S(1)} %get-tuple-element.8), channel_id=1, source_target_pairs={{16,0},{32,16},{48,32},{64,48},{80,64},{96,80},{112,96},{0,112},{1... | collective-permute-start | bytes 98312 | tf_op jit(solution)/shard_map/ppermute | solution.py:440
  6.4 2.7 %pack.1.refs_2_ = f32[16,48,8,128]{3,2,1,0:T(8,128)S(1)} custom-call(f32[8,64,512]{2,1,0:T(8,128)S(1)} %copy-done, f32[8,64,512]{2,1,0:T(8,128)S(1)} %copy-done.1, s32[64,512]{1,0:T(8,128)S(1)} %copy-done.2, s32[64,512]{1,0:T(8,128)S(1)} %copy-done.3), custom_call_target="tpu_custom_call" | custom-call | flops 20000000 | bytes 6000000 | tf_op jit(solution)/shard_map/pack/pallas_call | solution.py:147
  9.1 0.0 collective-permute-done.refs_0_
  9.1 0.0 collective-permute-done.1.refs_1_
  9.2 0.4 patch.1
  9.6 0.0 copy-start.4
  9.6 0.0 copy-start.5
  9.6 47.4 %all_to_all.10 = f32[16,48,8,128]{3,2,1,0:T(8,128)S(1)} all-to-all(f32[16,48,8,128]{3,2,1,0:T(8,128)S(1)} %patch.1), channel_id=1, replica_groups=mesh['gx'=8,'gy'=16] {'gy'}, dimensions={0} | all-to-all | bytes 6291456 | tf_op jit(solution)/shard_map/all_to_all | solution.py:443
  57.0 0.0 copy-done.4
  57.0 0.0 copy-done.5
  57.0 15.5 %sweeps.1 = f32[128,2,8,128]{3,2,1,0:T(8,128)S(1)} custom-call(s32[128]{0:T(128)S(1)} %copy-done.4, s32[128]{0:T(128)S(1)} %copy-done.5, f32[128,6,8,128]{3,2,1,0:T(8,128)S(1)} %bitcast.2), custom_call_target="tpu_custom_call" | custom-call | tf_op jit(solution)/shard_map/sweeps/pallas_call | solution.py:380
  72.5 20.1 %all_to_all.11.refs_0_ = f32[16,16,8,128]{3,2,1,0:T(8,128)S(1)} all-to-all(f32[16,16,8,128]{3,2,1,0:T(8,128)S(1)} %bitcast.3), channel_id=1, replica_groups=mesh['gx'=8,'gy'=16] {'gy'}, dimensions={0} | all-to-all | bytes 2097152 | tf_op jit(solution)/shard_map/all_to_all | solution.py:445
  92.6 1.8 %unpack.1 = f32[8,64,512]{2,1,0:T(8,128)} custom-call(f32[16,16,8,128]{3,2,1,0:T(8,128)S(1)} %all_to_all.11.refs_0_), custom_call_target="tpu_custom_call" | custom-call | tf_op jit(solution)/shard_map/unpack/pallas_call | solution.py:421
Async XLA Ops:
  0.0 1.2 %copy-start = (f32[8,64,512]{2,1,0:T(8,128)S(1)}, f32[8,64,512]{2,1,0:T(8,128)}, u32[]{:S(2)}) copy-start(f32[8,64,512]{2,1,0:T(8,128)} %refs_0_.2) | copy-start | bytes 3145732
  1.2 1.2 %copy-start.1 = (f32[8,64,512]{2,1,0:T(8,128)S(1)}, f32[8,64,512]{2,1,0:T(8,128)}, u32[]{:S(2)}) copy-start(f32[8,64,512]{2,1,0:T(8,128)} %refs_1_.2) | copy-start | bytes 3145732
  2.5 0.9 copy-start.2
  3.4 0.9 copy-start.3
  4.6 4.5 %collective-permute-start = (f32[64,128]{1,0:T(8,128)S(1)}, f32[64,128]{1,0:T(8,128)S(1)}, u32[]{:S(2)}, u32[]{:S(2)}) collective-permute-start(f32[64,128]{1,0:T(8,128)S(1)} %get-tuple-element.7), channel_id=1, source_target_pairs={{0,16},{16,32},{32,48},{48,64},{64,80},{80,96},{96,112},{112,0},{1... | collective-permute-start | bytes 98312 | tf_op jit(solution)/shard_map/ppermute | solution.py:439
  4.7 4.5 %collective-permute-start.1 = (f32[64,128]{1,0:T(8,128)S(1)}, f32[64,128]{1,0:T(8,128)S(1)}, u32[]{:S(2)}, u32[]{:S(2)}) collective-permute-start(f32[64,128]{1,0:T(8,128)S(1)} %get-tuple-element.8), channel_id=1, source_target_pairs={{16,0},{32,16},{48,32},{64,48},{80,64},{96,80},{112,96},{0,112},{1... | collective-permute-start | bytes 98312 | tf_op jit(solution)/shard_map/ppermute | solution.py:440
  9.6 47.5 %copy-start.4 = (s32[128]{0:T(128)S(1)}, s32[128]{0:T(128)}, u32[]{:S(2)}) copy-start(s32[128]{0:T(128)} %refs_0_.3) | copy-start | bytes 1540
  9.6 47.4 %copy-start.5 = (s32[128]{0:T(128)S(1)}, s32[128]{0:T(128)}, u32[]{:S(2)}) copy-start(s32[128]{0:T(128)} %refs_1_.3) | copy-start | bytes 1540

commit v4 on v3

--- a/solution.py
+++ b/solution.py
@@ -15,10 +15,12 @@
 PACK = 2
 UNPACK = 2
 SMALL = 12 * 1024 * 1024
+PLANES = 2 * K + 2
 UNIT = 4
+DEEPEST = 4
 GATHER = 11
 PHYSICS = 4
-FACES = 4
+FACES = 22
 SWEEP = 4
 LAST = 4
 
@@ -49,68 +51,52 @@
     return register % 3 + 3 * piece + (K if register >= 3 else 0)
 
 
-def edges_kernel(d_first, d_last, t_first, t_last, s_first, s_last, m_first, m_last, head_ref, tail_ref):
-    shape = (d_first.shape[1], LANES)
+def edges_kernel(first, last, head_ref, tail_ref):
+    shape = head_ref.shape
     lane = lane_of(shape)
-
-    def gather(density, tracer, mask, mixed, start):
+    for planes, start, out_ref in ((first, 0, head_ref), (last, LANES - HALO, tail_ref)):
         out = jnp.zeros(shape, jnp.float32)
-        for p in range(2 * K + 2):
-            if p < K:
-                plane = density[p]
-            elif p < 2 * K:
-                plane = tracer[p - K]
-            else:
-                plane = (mask if p == 2 * K else mixed)[...].astype(jnp.float32)
+        for p in range(PLANES):
             at = HALO * p
-            out = jnp.where((lane >= at) & (lane < at + HALO), rolled(plane, at - start), out)
-        return out
-
-    head_ref[...] = gather(d_first, t_first, s_first, m_first, 0)
-    tail_ref[...] = gather(d_last, t_last, s_last, m_last, LANES - HALO)
-
-
-def edges(density, tracer, mask, mixed):
-    rows, columns = mask.shape
+            out = jnp.where((lane >= at) & (lane < at + HALO), rolled(planes[p], at - start), out)
+        out_ref[...] = out
+
+
+def edges(planes):
+    rows, columns = planes.shape[1:]
     last = columns // LANES - 1
-    cube = lambda c: pl.BlockSpec((K, rows, LANES), lambda i: (0, 0, c))
-    flat = lambda c: pl.BlockSpec((rows, LANES), lambda i: (0, c))
+    rim = pl.BlockSpec((rows, LANES), lambda i: (0, 0))
     out = jax.ShapeDtypeStruct((rows, LANES), jnp.float32)
-    rim = pl.BlockSpec((rows, LANES), lambda i: (0, 0))
     return pl.pallas_call(
         edges_kernel,
         grid=(1,),
         out_shape=(out, out),
+        in_specs=[
+            pl.BlockSpec((PLANES, rows, LANES), lambda i: (0, 0, 0)),
+            pl.BlockSpec((PLANES, rows, LANES), lambda i: (0, 0, last)),
+        ],
         out_specs=(rim, rim),
         compiler_params=pltpu.CompilerParams(vmem_limit_bytes=SMALL),
-        in_specs=[cube(0), cube(last), cube(0), cube(last), flat(0), flat(last), flat(0), flat(last)],
         name="edges",
-    )(density, density, tracer, tracer, mask, mask, mixed, mixed)
-
-
-def pack_kernel(width, density, tracer, mask, mixed, out_ref):
+    )(planes, planes)
+
+
+def pack_kernel(width, planes, out_ref):
     piece = width + 2 * HALO
     per_tile = LANES // width
-    tiles = mask.shape[1] // LANES
-    count = mask.shape[0] // BR
+    tiles = planes.shape[2] // LANES
+    count = planes.shape[1] // BR
     lane = lane_of()
 
     def columns(p, row):
-        for t in range(tiles):
-            at = slice(LANES * t, LANES * (t + 1))
-            if p < K:
-                yield density[p, row, at]
-            elif p < 2 * K:
-                yield tracer[p - K, row, at]
-            else:
-                yield (mask if p == 2 * K else mixed)[row, at].astype(jnp.float32)
+        return [planes[p, row, LANES * t : LANES * (t + 1)] for t in range(tiles)]
 
     for u in range(count):
         block = pl.program_id(0) * count + u
         for v in range(VREGS):
             whole, seam = [], []
             for m in range(SLOTS):
-                own = list(columns(plane_at(v, m), slice(BR * u, BR * (u + 1))))
+                own = columns(plane_at(v, m), slice(BR * u, BR * (u + 1)))
                 whole.append(own)
                 seam.append(
                     [own[0]]
@@ -133,13 +119,10 @@
                 )
 
 
-def pack(density, tracer, mask, mixed, strips):
-    rows, columns = mask.shape
+def pack(planes, strips):
+    rows, columns = planes.shape[1:]
     blocks = rows // BR
     width = columns // strips
-    tall = rows // PACK
-    cube = pl.BlockSpec((K, tall, columns), lambda b: (0, b, 0))
-    flat = pl.BlockSpec((tall, columns), lambda b: (b, 0))
 
     def kernel(*refs):
         pack_kernel(width, *refs)
@@ -148,12 +131,12 @@
         kernel,
         grid=(PACK,),
         out_shape=jax.ShapeDtypeStruct((strips, blocks * VREGS, BR, LANES), jnp.float32),
-        in_specs=[cube, cube, flat, flat],
+        in_specs=[pl.BlockSpec((PLANES, rows // PACK, columns), lambda b: (0, b, 0))],
         out_specs=pl.BlockSpec(memory_space=pltpu.VMEM),
         compiler_params=pltpu.CompilerParams(vmem_limit_bytes=SMALL),
         cost_estimate=pl.CostEstimate(flops=20000000, bytes_accessed=6000000, transcendentals=0),
         name="pack",
-    )(density, tracer, mask, mixed)
+    )(planes)
 
 
 def patch_kernel(piece, west, east, packed, out_ref):
@@ -273,28 +256,29 @@
             sum_e = east * (rolled(f[k], -1) - f[k]) + west * (f[k] - rolled(f[k], 1))
             sum_n = north * (rho[k, up, :] - f[k]) + south * (f[k] - rho[k, down, :])
             above, under = max(k - 1, 0), min(k + 1, K - 1)
-            rising = 0.5 * STRATIFICATION * (under - above)
-            denominator = jnp.maximum(0.5 * (f[under] - f[above]) + rising, DENSITY_FLOOR)
-            scale = -0.5 / denominator
+            rising = STRATIFICATION * (under - above)
+            twice = jnp.maximum((f[under] - f[above]) + rising, 2.0 * DENSITY_FLOOR)
+            scale = 1.0 / twice
             se = sum_e * scale
             sn = sum_n * scale
             squared = se * se + sn * sn
-            taper = 0.5 + 0.5 * jnp.tanh((SLOPE_LIMIT - squared) * (1.0 / TAPER_WIDTH))
-            factor = taper * jnp.minimum(1.0, (k + 1.0) * per_mixed) * here
-            se = se * factor
-            sn = sn * factor
-            squared = se * se + sn * sn
-            root = jnp.sqrt(denominator * (squared + KERNEL_OFFSET))
-            total += jnp.where(mixed <= float(k), root, 0.0)
-            cp[k, at, :] = se
-            cq[k, at, :] = sn
+            taper = 0.5 + 0.5 * jnp.tanh(SLOPE_LIMIT / TAPER_WIDTH - squared * (1.0 / TAPER_WIDTH))
+            if k < DEEPEST:
+                taper = taper * jnp.minimum(1.0, (k + 1.0) * per_mixed)
+            squared = squared * (taper * taper)
+            under_root = twice * (squared + KERNEL_OFFSET)
+            root = under_root * lax.rsqrt(under_root)
+            total += jnp.where(mixed <= float(k), root, 0.0) if k < DEEPEST else root
+            cp[k, at, :] = se * taper
+            cq[k, at, :] = sn * taper
             kept.append(squared)
-        kappa = here * (BASE_DIFFUSIVITY + VISBECK_ALPHA * total / (K - mixed))
+        share = (VISBECK_ALPHA * 0.5**0.5) * total / (K - mixed)
+        kappa = here * (BASE_DIFFUSIVITY + share)
         kap[at, :] = kappa
         weight = (0.5 * TIME_STEP) * kappa
         for k in range(K):
-            cp[k, at, :] = weight * cp[k, at, :]
-            cq[k, at, :] = weight * cq[k, at, :]
+            cp[k, at, :] = -weight * cp[k, at, :]
+            cq[k, at, :] = -weight * cq[k, at, :]
             cr[k, at, :] = (0.5 * weight) * kept[k]
 
     loop(physics, depth, PHYSICS)
@@ -350,9 +334,11 @@
     per_out = LANES // width
     wide = lane_of((BR * LAST, LANES))
 
-    def last(back):
-        c = depth // LAST - 1 - back
-        result = advance(c, source, LAST)
+    target = tb if source is ta else ta
+    chunks = depth // LAST
+
+    def repack(c):
+        result = [target[k, rows(c, 0, LAST), :] for k in range(K)]
         for g in reversed(range(SLOTS)):
             for h in range(K // per_out):
                 value = None
@@ -363,7 +349,19 @@
                     t = owner[slot_of[c * LAST + u + depth * g]]
                     out_ref[t, h] = value[BR * u : BR * (u + 1), :]
 
-    loop(last, depth, LAST)
+    def final(c):
+        result = advance(c, source, LAST)
+        for k in range(K):
+            target[k, rows(c, 0, LAST), :] = result[k]
+
+    def last(back, carry):
+        repack(chunks - back)
+        final(chunks - 1 - back)
+        return carry
+
+    final(chunks - 1)
+    lax.fori_loop(1, chunks, last, 0)
+    repack(0)
 
 
 def sweeps(order, owner, got, width):
@@ -435,10 +433,12 @@
     ring = lax.axis_size("gx")
     width = columns // strips
     blocks = rows // BR
-    head, tail = edges(density, tracer, sea_mask, mixed_level)
+    flats = [flat[None].astype(jnp.float32) for flat in (sea_mask, mixed_level)]
+    planes = jnp.concatenate([density, tracer, *flats])
+    head, tail = edges(planes)
     west = lax.ppermute(tail, "gx", [(i, (i + 1) % ring) for i in range(ring)])
     east = lax.ppermute(head, "gx", [((i + 1) % ring, i) for i in range(ring)])
-    packed = pack(density, tracer, sea_mask, mixed_level, strips)
+    packed = pack(planes, strips)
     packed = patch(west, east, packed, width + 2 * HALO)
     got = lax.all_to_all(packed, "gy", split_axis=0, concat_axis=0, tiled=True)
     done = sweeps(tile_blocks, block_owner, got.reshape(strips * blocks, VREGS, BR, LANES), width)

time: 94.7 us -> 91.5 us (0.966)
  local copies, waits for them, and re-layouts: 4.27 us -> 0.01 us
  other arithmetic: 0 us -> 2.73 us
  Pallas kernels: 20.8 us -> 19.2 us
    unnamed x12 -> x4, local copies, waits for them, and re-layouts: 4.27 us -> 0.01 us
    concatenate x0 -> x1, other arithmetic: none -> 1.75 us  [on_device(): planes = jnp.concatenate([density, tracer, *flats])]
    pallas_call x1, Pallas kernels: 15.5 us -> 13.9 us  [sweeps(): pl.pallas_call(kernel, out_shape=jax.ShapeDtypeStruct((blocks, outs, BR,...]
    convert_element_type x0 -> x1, other arithmetic: none -> 0.99 us  [on_device(): flats = [flat[None].astype(jnp.float32) for flat in (sea_mask, mixed_level)]]
where the time goes in v4:
time: 91.5 us; the launch traced here: 91.3 us
  blocking collectives  67.5 us (74%)
  Pallas kernels  19.2 us (21%)
  other arithmetic  2.73 us (3%)
  starting transfers between devices  1.75 us (2%)
    all_to_all x1, blocking collectives, on_device(): got = lax.all_to_all(packed, 'gy', split_axis=0, concat_axis=0, tiled=True)  47.4 us
    all_to_all x1, blocking collectives, on_device(): lax.all_to_all(done.reshape(strips, -1, BR, LANES), 'gy', split_axis=0, c...  20.1 us
    pallas_call x1, Pallas kernels, sweeps(): pl.pallas_call(kernel, out_shape=jax.ShapeDtypeStruct((blocks, outs, BR,...  13.9 us
    pallas_call x1, Pallas kernels, pack(): pl.pallas_call(kernel, grid=(PACK,), out_shape=jax.ShapeDtypeStruct((stri...  2.76 us
  transfers between devices with their start and end apart: 2, of which 0 were waited for; matrix products, arithmetic and copies ran while one was open for 0% of the time, Pallas kernels for 3%

profile of v4, /device:TPU:32, one launch (start us, length us, event | category | flops | bytes accessed | tf_op | source)
XLA Modules:
  0.0 91.3 jit_solution(14724083639590385645)
XLA Ops:
  0.0 1.0 %convert_bitcast_fusion = (f32[1,64,512]{2,1,0:T(8,128)S(1)}, f32[1,64,512]{2,1,0:T(8,128)S(1)}) fusion(s32[64,512]{1,0:T(8,128)} %param.9, s32[64,512]{1,0:T(8,128)} %param.8), kind=kLoop, calls=%fused_computation.1 | loop fusion | flops 65536 | bytes 524288 | tf_op jit(solution)/shard_map/convert_element_type | solution.py:436
  1.0 1.7 %pad_maximum_fusion.first.last.refs_0_ = f32[18,64,512]{2,1,0:T(8,128)S(1)} fusion(f32[1,64,512]{2,1,0:T(8,128)S(1)} %get-tuple-element.9, f32[1,64,512]{2,1,0:T(8,128)S(1)} %get-tuple-element.10, f32[8,64,512]{2,1,0:T(8,128)} %param.7, f32[8,64,512]{2,1,0:T(8,128)} %param.6), kind=kLoop, calls=%fused_computation | loop fusion | flops 1769472 | bytes 4718592 | tf_op jit(solution)/shard_map/concatenate | solution.py:437
  2.7 0.4 edges.1
  3.1 0.0 collective-permute-start
  3.1 1.7 %collective-permute-start.1 = (f32[64,128]{1,0:T(8,128)S(1)}, f32[64,128]{1,0:T(8,128)S(1)}, u32[]{:S(2)}, u32[]{:S(2)}) collective-permute-start(f32[64,128]{1,0:T(8,128)S(1)} %get-tuple-element.8), channel_id=1, source_target_pairs={{16,0},{32,16},{48,32},{64,48},{80,64},{96,80},{112,96},{0,112},{1... | collective-permute-start | bytes 98312 | tf_op jit(solution)/shard_map/ppermute | solution.py:440
  4.9 2.8 %pack.1.refs_2_ = f32[16,48,8,128]{3,2,1,0:T(8,128)S(1)} custom-call(f32[18,64,512]{2,1,0:T(8,128)S(1)} %pad_maximum_fusion.first.last.refs_0_), custom_call_target="tpu_custom_call" | custom-call | flops 20000000 | bytes 6000000 | tf_op jit(solution)/shard_map/pack/pallas_call | solution.py:130
  7.6 0.0 collective-permute-done.refs_0_
  7.7 0.0 collective-permute-done.1.refs_1_
  7.7 0.4 patch.1
  8.1 0.0 copy-start
  8.1 0.0 copy-start.1
  8.1 47.4 %all_to_all.10 = f32[16,48,8,128]{3,2,1,0:T(8,128)S(1)} all-to-all(f32[16,48,8,128]{3,2,1,0:T(8,128)S(1)} %patch.1), channel_id=1, replica_groups=mesh['gx'=8,'gy'=16] {'gy'}, dimensions={0} | all-to-all | bytes 6291456 | tf_op jit(solution)/shard_map/all_to_all | solution.py:443
  55.5 0.0 copy-done
  55.5 0.0 copy-done.1
  55.5 13.9 %sweeps.1 = f32[128,2,8,128]{3,2,1,0:T(8,128)S(1)} custom-call(s32[128]{0:T(128)S(1)} %copy-done, s32[128]{0:T(128)S(1)} %copy-done.1, f32[128,6,8,128]{3,2,1,0:T(8,128)S(1)} %bitcast.6), custom_call_target="tpu_custom_call" | custom-call | tf_op jit(solution)/shard_map/sweeps/pallas_call | solution.py:378
  69.4 20.1 %all_to_all.11.refs_0_ = f32[16,16,8,128]{3,2,1,0:T(8,128)S(1)} all-to-all(f32[16,16,8,128]{3,2,1,0:T(8,128)S(1)} %bitcast.7), channel_id=1, replica_groups=mesh['gx'=8,'gy'=16] {'gy'}, dimensions={0} | all-to-all | bytes 2097152 | tf_op jit(solution)/shard_map/all_to_all | solution.py:445
  89.5 1.8 %unpack.1 = f32[8,64,512]{2,1,0:T(8,128)} custom-call(f32[16,16,8,128]{3,2,1,0:T(8,128)S(1)} %all_to_all.11.refs_0_), custom_call_target="tpu_custom_call" | custom-call | tf_op jit(solution)/shard_map/unpack/pallas_call | solution.py:419
Async XLA Ops:
  3.1 4.5 %collective-permute-start = (f32[64,128]{1,0:T(8,128)S(1)}, f32[64,128]{1,0:T(8,128)S(1)}, u32[]{:S(2)}, u32[]{:S(2)}) collective-permute-start(f32[64,128]{1,0:T(8,128)S(1)} %get-tuple-element.7), channel_id=1, source_target_pairs={{0,16},{16,32},{32,48},{48,64},{64,80},{80,96},{96,112},{112,0},{1... | collective-permute-start | bytes 98312 | tf_op jit(solution)/shard_map/ppermute | solution.py:439
  3.1 4.5 %collective-permute-start.1 = (f32[64,128]{1,0:T(8,128)S(1)}, f32[64,128]{1,0:T(8,128)S(1)}, u32[]{:S(2)}, u32[]{:S(2)}) collective-permute-start(f32[64,128]{1,0:T(8,128)S(1)} %get-tuple-element.8), channel_id=1, source_target_pairs={{16,0},{32,16},{48,32},{64,48},{80,64},{96,80},{112,96},{0,112},{1... | collective-permute-start | bytes 98312 | tf_op jit(solution)/shard_map/ppermute | solution.py:440
  8.1 47.4 %copy-start = (s32[128]{0:T(128)S(1)}, s32[128]{0:T(128)}, u32[]{:S(2)}) copy-start(s32[128]{0:T(128)} %refs_0_.1) | copy-start | bytes 1540
  8.1 47.4 %copy-start.1 = (s32[128]{0:T(128)S(1)}, s32[128]{0:T(128)}, u32[]{:S(2)}) copy-start(s32[128]{0:T(128)} %refs_1_.1) | copy-start | bytes 1540

commit v5 on v4

--- a/solution.py
+++ b/solution.py
@@ -12,13 +12,12 @@
 LANES = 128
 SLOTS = 3
 VREGS = 6
-PACK = 2
 UNPACK = 2
 SMALL = 12 * 1024 * 1024
 PLANES = 2 * K + 2
 UNIT = 4
 DEEPEST = 4
-GATHER = 11
+GATHER = 4
 PHYSICS = 4
 FACES = 22
 SWEEP = 4
@@ -51,77 +50,76 @@
     return register % 3 + 3 * piece + (K if register >= 3 else 0)
 
 
-def edges_kernel(first, last, head_ref, tail_ref):
+def edges_kernel(planes, head_ref, tail_ref):
     shape = head_ref.shape
     lane = lane_of(shape)
-    for planes, start, out_ref in ((first, 0, head_ref), (last, LANES - HALO, tail_ref)):
+    last = planes.shape[2] - LANES
+    for start, edge, out_ref in ((0, 0, head_ref), (last, LANES - HALO, tail_ref)):
         out = jnp.zeros(shape, jnp.float32)
         for p in range(PLANES):
             at = HALO * p
-            out = jnp.where((lane >= at) & (lane < at + HALO), rolled(planes[p], at - start), out)
+            plane = rolled(planes[p, :, start : start + LANES], at - edge)
+            out = jnp.where((lane >= at) & (lane < at + HALO), plane, out)
         out_ref[...] = out
 
 
 def edges(planes):
-    rows, columns = planes.shape[1:]
-    last = columns // LANES - 1
-    rim = pl.BlockSpec((rows, LANES), lambda i: (0, 0))
-    out = jax.ShapeDtypeStruct((rows, LANES), jnp.float32)
+    whole = pl.BlockSpec(memory_space=pltpu.VMEM)
+    out = jax.ShapeDtypeStruct((planes.shape[1], LANES), jnp.float32)
     return pl.pallas_call(
         edges_kernel,
-        grid=(1,),
         out_shape=(out, out),
-        in_specs=[
-            pl.BlockSpec((PLANES, rows, LANES), lambda i: (0, 0, 0)),
-            pl.BlockSpec((PLANES, rows, LANES), lambda i: (0, 0, last)),
-        ],
-        out_specs=(rim, rim),
+        in_specs=[whole],
+        out_specs=(whole, whole),
         compiler_params=pltpu.CompilerParams(vmem_limit_bytes=SMALL),
         name="edges",
-    )(planes, planes)
+    )(planes)
 
 
 def pack_kernel(width, planes, out_ref):
     piece = width + 2 * HALO
     per_tile = LANES // width
     tiles = planes.shape[2] // LANES
-    count = planes.shape[1] // BR
     lane = lane_of()
 
-    def columns(p, row):
-        return [planes[p, row, LANES * t : LANES * (t + 1)] for t in range(tiles)]
-
-    for u in range(count):
-        block = pl.program_id(0) * count + u
+    def below(limit, start):
+        return ((lane - start) & (LANES - 1)) < limit
+
+    west_half = [below(LANES // 2, piece * m) for m in range(SLOTS)]
+    one = [below(piece, width * q - HALO) for q in range(per_tile)]
+    two = [below(2 * piece, width * q - HALO) for q in range(per_tile)]
+
+    for b in range(planes.shape[1] // BR):
         for v in range(VREGS):
             whole, seam = [], []
             for m in range(SLOTS):
-                own = columns(plane_at(v, m), slice(BR * u, BR * (u + 1)))
+                own = [
+                    rolled(
+                        planes[plane_at(v, m), BR * b : BR * (b + 1), LANES * t : LANES * (t + 1)],
+                        piece * m,
+                    )
+                    for t in range(tiles)
+                ]
                 whole.append(own)
                 seam.append(
                     [own[0]]
-                    + [jnp.where(lane < LANES // 2, own[t], own[t - 1]) for t in range(1, tiles)]
+                    + [jnp.where(west_half[m], own[t], own[t - 1]) for t in range(1, tiles)]
                     + [own[-1]]
                 )
             for j in range(tiles * per_tile):
                 t, q = divmod(j, per_tile)
-                parts = []
-                for m in range(SLOTS):
-                    if q == 0:
-                        source = seam[m][t]
-                    elif q == per_tile - 1:
-                        source = seam[m][t + 1]
-                    else:
-                        source = whole[m][t]
-                    parts.append(rolled(source, piece * m - (width * q - HALO)))
-                out_ref[j, block * VREGS + v] = jnp.where(
-                    lane < piece, parts[0], jnp.where(lane < 2 * piece, parts[1], parts[2])
-                )
+                if q == 0:
+                    parts = [seam[m][t] for m in range(SLOTS)]
+                elif q == per_tile - 1:
+                    parts = [seam[m][t + 1] for m in range(SLOTS)]
+                else:
+                    parts = [whole[m][t] for m in range(SLOTS)]
+                out_ref[j, b * VREGS + v] = jnp.where(one[q], parts[0], jnp.where(two[q], parts[1], parts[2]))
 
 
 def pack(planes, strips):
     rows, columns = planes.shape[1:]
-    blocks = rows // BR
+    whole = pl.BlockSpec(memory_space=pltpu.VMEM)
     width = columns // strips
 
     def kernel(*refs):
@@ -129,41 +127,40 @@
 
     return pl.pallas_call(
         kernel,
-        grid=(PACK,),
-        out_shape=jax.ShapeDtypeStruct((strips, blocks * VREGS, BR, LANES), jnp.float32),
-        in_specs=[pl.BlockSpec((PLANES, rows // PACK, columns), lambda b: (0, b, 0))],
-        out_specs=pl.BlockSpec(memory_space=pltpu.VMEM),
+        out_shape=jax.ShapeDtypeStruct((strips, rows // BR * VREGS, BR, LANES), jnp.float32),
+        in_specs=[whole],
+        out_specs=whole,
         compiler_params=pltpu.CompilerParams(vmem_limit_bytes=SMALL),
         cost_estimate=pl.CostEstimate(flops=20000000, bytes_accessed=6000000, transcendentals=0),
         name="pack",
     )(planes)
 
 
-def patch_kernel(piece, west, east, packed, out_ref):
+def patch_kernel(width, west, east, packed, out_ref):
+    piece = width + 2 * HALO
     lane = lane_of()
     strips = packed.shape[0]
-    blocks = west.shape[0] // BR
 
     def fill(b, strip, edge, start):
-        rim = edge[pl.ds(pl.multiple_of(BR * b, BR), BR), :]
+        rim = edge[BR * b : BR * (b + 1), :]
         for v in range(VREGS):
             value = packed[strip, b * VREGS + v]
             for m in range(SLOTS):
-                at = piece * m + start
+                at = (piece * m + start) % LANES
                 here = (lane >= at) & (lane < at + HALO)
                 value = jnp.where(here, rolled(rim, at - HALO * plane_at(v, m)), value)
             out_ref[strip, b * VREGS + v] = value
 
-    for b in range(blocks):
-        fill(b, 0, west, 0)
-        fill(b, strips - 1, east, piece - HALO)
-
-
-def patch(west, east, packed, piece):
+    for b in range(west.shape[0] // BR):
+        fill(b, 0, west, LANES - HALO)
+        fill(b, strips - 1, east, 0)
+
+
+def patch(west, east, packed, width):
     whole = pl.BlockSpec(memory_space=pltpu.VMEM)
 
     def kernel(*refs):
-        patch_kernel(piece, *refs)
+        patch_kernel(width, *refs)
 
     return pl.pallas_call(
         kernel,
@@ -181,7 +178,12 @@
 ):
     piece = width + 2 * HALO
     depth = (sea.shape[0] - 2 * BR) // BR
-    lane = lane_of()
+    strip = lax.axis_index("gy") % (LANES // width)
+
+    def lane_from(start, shape=(BR, LANES)):
+        return (lane_of(shape) - (width * strip + (start - HALO))) & (LANES - 1)
+
+    lane = lane_from(0)
     first = lane < piece
     second = lane < 2 * piece
 
@@ -211,6 +213,9 @@
         bottom = jnp.where(second, rolled(ref[pl.ds(BR, BR), :], -piece), 0.0)
         ref[pl.ds(0, BR), :] = top
         ref[pl.ds(BR * (depth + 1), BR), :] = bottom
+
+    one = [lane_from(piece * n) < piece for n in range(SLOTS)]
+    two = [lane_from(piece * n) < 2 * piece for n in range(SLOTS)]
 
     def gather(c):
         for u in range(GATHER):
@@ -218,17 +223,26 @@
             slots = [slot_of[i + depth * m] for m in range(SLOTS)]
             owners = [owner[s] for s in slots]
             real = jnp.where(i + depth * (SLOTS - 1) < blocks, 1.0, 0.0)
-
-            def plane(v, n, where):
-                parts = [rolled(got[where[m], v], piece * (m - n)) for m in range(SLOTS)]
-                return jnp.where(first, parts[0], jnp.where(second, parts[1], parts[2] * real))
-
             at = rows(i)
-            for k in range(K):
-                rho[k, at, :] = plane(k % 3, k // 3, slots)
-                ta[k, at, :] = plane(3 + k % 3, k // 3, owners)
-            sea[at, :] = plane(2, 2, slots)
-            mix[at, :] = plane(5, 2, slots)
+            for v in range(VREGS):
+                where = slots if v < 3 else owners
+                parts = [got[where[m], v] for m in range(SLOTS)]
+                parts[2] = parts[2] * real
+                parts = [rolled(parts[m], piece * m) for m in range(SLOTS)]
+                for n in range(SLOTS):
+                    plane = jnp.where(one[n], parts[0], jnp.where(two[n], parts[1], parts[2]))
+                    plane = rolled(plane, -piece * n)
+                    p = plane_at(v, n)
+                    if p < K:
+                        rho[p, at, :] = plane
+                    elif p < 2 * K:
+                        ta[p - K, at, :] = plane
+                    elif p == 2 * K:
+                        sea[at, :] = plane
+            levels = [got[slots[m], 5] for m in range(SLOTS)]
+            levels[2] = levels[2] * real
+            levels = [rolled(levels[m], piece * m) for m in range(SLOTS)]
+            mix[at, :] = rolled(jnp.where(one[2], levels[0], jnp.where(two[2], levels[1], levels[2])), -2 * piece)
 
     loop(gather, depth, GATHER)
     for k in range(K):
@@ -332,19 +346,22 @@
         sweep(*((ta, tb) if n % 2 == 0 else (tb, ta)))
     source = ta if (ITERS - 1) % 2 == 0 else tb
     per_out = LANES // width
-    wide = lane_of((BR * LAST, LANES))
 
     target = tb if source is ta else ta
     chunks = depth // LAST
 
+    inner = [lane_from(piece * g + HALO, (BR * LAST, LANES)) for g in range(SLOTS)]
+
     def repack(c):
-        result = [target[k, rows(c, 0, LAST), :] for k in range(K)]
-        for g in reversed(range(SLOTS)):
-            for h in range(K // per_out):
-                value = None
-                for m in range(per_out):
-                    part = rolled(result[h * per_out + m], width * m - (piece * g + HALO))
-                    value = part if m == 0 else jnp.where(wide < width * m, value, part)
+        for h in range(K // per_out):
+            levels = [
+                rolled(target[h * per_out + m, rows(c, 0, LAST), :], width * m) for m in range(per_out)
+            ]
+            for g in reversed(range(SLOTS)):
+                value = levels[-1]
+                for m in reversed(range(per_out - 1)):
+                    value = jnp.where(inner[g] < width * (m + 1), levels[m], value)
+                value = rolled(value, -piece * g)
                 for u in range(LAST):
                     t = owner[slot_of[c * LAST + u + depth * g]]
                     out_ref[t, h] = value[BR * u : BR * (u + 1), :]
@@ -395,17 +412,19 @@
     tiles = out_ref.shape[2] // LANES
     count = out_ref.shape[1] // BR
     outs = K // per_tile
-    lane = lane_of()
+    place = lane_of() // width
     for u in range(count):
         block = pl.program_id(0) * count + u
-        for k in range(K):
-            h, m = divmod(k, per_tile)
+        for h in range(outs):
             for t in range(tiles):
-                value = None
-                for q in range(per_tile):
-                    part = rolled(got[t * per_tile + q, block * outs + h], width * (q - m))
-                    value = part if q == 0 else jnp.where(lane < width * q, value, part)
-                out_ref[k, BR * u : BR * (u + 1), LANES * t : LANES * (t + 1)] = value
+                strips = [got[t * per_tile + q, block * outs + h] for q in range(per_tile)]
+                for m in range(per_tile):
+                    value = strips[-1]
+                    for q in range(per_tile - 1):
+                        value = jnp.where(place == (m + q) % per_tile, strips[q], value)
+                    out_ref[
+                        h * per_tile + m, BR * u : BR * (u + 1), LANES * t : LANES * (t + 1)
+                    ] = rolled(value, -width * m)
 
 
 def unpack(got, rows, columns):
@@ -439,7 +458,7 @@
     west = lax.ppermute(tail, "gx", [(i, (i + 1) % ring) for i in range(ring)])
     east = lax.ppermute(head, "gx", [((i + 1) % ring, i) for i in range(ring)])
     packed = pack(planes, strips)
-    packed = patch(west, east, packed, width + 2 * HALO)
+    packed = patch(west, east, packed, width)
     got = lax.all_to_all(packed, "gy", split_axis=0, concat_axis=0, tiled=True)
     done = sweeps(tile_blocks, block_owner, got.reshape(strips * blocks, VREGS, BR, LANES), width)
     back = lax.all_to_all(

time: 91.5 us -> 90.4 us (0.988)
  Pallas kernels: 19.2 us -> 16.2 us
  waiting for transfers between devices: 0.01 us -> 1.02 us
    pallas_call x2, Pallas kernels: 3.12 us -> 0.93 us  [the longest x1 0.57 us: pack(): pl.pallas_call(kernel, out_shape=jax.ShapeDtypeStruct((strips, rows // BR...]
    all_to_all x1, blocking collectives: 20.1 us -> 22 us  [on_device(): lax.all_to_all(done.reshape(strips, -1, BR, LANES), 'gy', split_axis=0, c...]
    all_to_all x1, blocking collectives: 47.4 us -> 46.2 us  [on_device(): got = lax.all_to_all(packed, 'gy', split_axis=0, concat_axis=0, tiled=True)]
    ppermute x1, waiting for transfers between devices: 0.01 us -> 1.02 us  [on_device(): west = lax.ppermute(tail, 'gx', [(i, (i + 1) % ring) for i in range(ring)])]
  transfers between devices with their start and end apart: 2 -> 2, of which waited for: 0 -> 1; matrix products, arithmetic and copies ran while one was open for 0% -> 0% of each run, Pallas kernels for 3% -> 1%
where the time goes in v5:
time: 90.4 us; the launch traced here: 90 us
  blocking collectives  68.2 us (75%)
  Pallas kernels  16.2 us (18%)
  other arithmetic  2.73 us (3%)
  starting transfers between devices  1.75 us (2%)
  waiting for transfers between devices  1.02 us (1%)
    all_to_all x1, blocking collectives, on_device(): got = lax.all_to_all(packed, 'gy', split_axis=0, concat_axis=0, tiled=True)  46.2 us
    all_to_all x1, blocking collectives, on_device(): lax.all_to_all(done.reshape(strips, -1, BR, LANES), 'gy', split_axis=0, c...  22 us
    pallas_call x1, Pallas kernels, sweeps(): pl.pallas_call(kernel, out_shape=jax.ShapeDtypeStruct((blocks, outs, BR,...  13.7 us
  transfers between devices with their start and end apart: 2, of which 1 were waited for; matrix products, arithmetic and copies ran while one was open for 0% of the time, Pallas kernels for 1%

profile of v5, /device:TPU:32, one launch (start us, length us, event | category | flops | bytes accessed | tf_op | source)
XLA Modules:
  0.0 90.0 jit_solution(3202216849377121057)
XLA Ops:
  0.0 1.0 %convert_bitcast_fusion = (f32[1,64,512]{2,1,0:T(8,128)S(1)}, f32[1,64,512]{2,1,0:T(8,128)S(1)}) fusion(s32[64,512]{1,0:T(8,128)} %param.9, s32[64,512]{1,0:T(8,128)} %param.8), kind=kLoop, calls=%fused_computation.1 | loop fusion | flops 65536 | bytes 524288 | tf_op jit(solution)/shard_map/convert_element_type | solution.py:455
  1.0 1.7 %pad_maximum_fusion.planes.refs_0_ = f32[18,64,512]{2,1,0:T(8,128)S(1)} fusion(f32[1,64,512]{2,1,0:T(8,128)S(1)} %get-tuple-element.9, f32[1,64,512]{2,1,0:T(8,128)S(1)} %get-tuple-element.10, f32[8,64,512]{2,1,0:T(8,128)} %param.7, f32[8,64,512]{2,1,0:T(8,128)} %param.6), kind=kLoop, calls=%fused_computation | loop fusion | flops 1769472 | bytes 4718592 | tf_op jit(solution)/shard_map/concatenate | solution.py:456
  2.7 0.4 edges.1
  3.1 0.0 collective-permute-start
  3.1 1.7 %collective-permute-start.1 = (f32[64,128]{1,0:T(8,128)S(1)}, f32[64,128]{1,0:T(8,128)S(1)}, u32[]{:S(2)}, u32[]{:S(2)}) collective-permute-start(f32[64,128]{1,0:T(8,128)S(1)} %get-tuple-element.8), channel_id=1, source_target_pairs={{16,0},{32,16},{48,32},{64,48},{80,64},{96,80},{112,96},{0,112},{1... | collective-permute-start | bytes 98312 | tf_op jit(solution)/shard_map/ppermute | solution.py:459
  4.9 0.6 pack.1.refs_2_
  5.4 1.0 %collective-permute-done.refs_0_ = f32[64,128]{1,0:T(8,128)S(1)} collective-permute-done((f32[64,128]{1,0:T(8,128)S(1)}, f32[64,128]{1,0:T(8,128)S(1)}, u32[]{:S(2)}, u32[]{:S(2)}) %collective-permute-start) | collective-permute-done | bytes 32800 | tf_op jit(solution)/shard_map/ppermute | solution.py:458
  6.5 0.0 collective-permute-done.1.refs_1_
  6.5 0.4 patch.1
  6.9 0.0 copy-start
  6.9 0.0 copy-start.1
  6.9 46.2 %all_to_all.10 = f32[16,48,8,128]{3,2,1,0:T(8,128)S(1)} all-to-all(f32[16,48,8,128]{3,2,1,0:T(8,128)S(1)} %patch.1), channel_id=1, replica_groups=mesh['gx'=8,'gy'=16] {'gy'}, dimensions={0} | all-to-all | bytes 6291456 | tf_op jit(solution)/shard_map/all_to_all | solution.py:462
  53.1 0.0 copy-done
  53.1 0.0 copy-done.1
  53.1 13.7 %sweeps.1 = f32[128,2,8,128]{3,2,1,0:T(8,128)S(1)} custom-call(s32[128]{0:T(128)S(1)} %copy-done, s32[128]{0:T(128)S(1)} %copy-done.1, f32[128,6,8,128]{3,2,1,0:T(8,128)S(1)} %bitcast.6), custom_call_target="tpu_custom_call" | custom-call | tf_op jit(solution)/shard_map/sweeps/pallas_call | solution.py:395
  66.9 22.0 %all_to_all.11.refs_0_ = f32[16,16,8,128]{3,2,1,0:T(8,128)S(1)} all-to-all(f32[16,16,8,128]{3,2,1,0:T(8,128)S(1)} %bitcast.7), channel_id=1, replica_groups=mesh['gx'=8,'gy'=16] {'gy'}, dimensions={0} | all-to-all | bytes 2097152 | tf_op jit(solution)/shard_map/all_to_all | solution.py:464
  88.9 1.1 %unpack.1 = f32[8,64,512]{2,1,0:T(8,128)} custom-call(f32[16,16,8,128]{3,2,1,0:T(8,128)S(1)} %all_to_all.11.refs_0_), custom_call_target="tpu_custom_call" | custom-call | tf_op jit(solution)/shard_map/unpack/pallas_call | solution.py:438
Async XLA Ops:
  3.1 3.4 %collective-permute-start = (f32[64,128]{1,0:T(8,128)S(1)}, f32[64,128]{1,0:T(8,128)S(1)}, u32[]{:S(2)}, u32[]{:S(2)}) collective-permute-start(f32[64,128]{1,0:T(8,128)S(1)} %get-tuple-element.7), channel_id=1, source_target_pairs={{0,16},{16,32},{32,48},{48,64},{64,80},{80,96},{96,112},{112,0},{1... | collective-permute-start | bytes 98312 | tf_op jit(solution)/shard_map/ppermute | solution.py:458
  3.1 3.3 %collective-permute-start.1 = (f32[64,128]{1,0:T(8,128)S(1)}, f32[64,128]{1,0:T(8,128)S(1)}, u32[]{:S(2)}, u32[]{:S(2)}) collective-permute-start(f32[64,128]{1,0:T(8,128)S(1)} %get-tuple-element.8), channel_id=1, source_target_pairs={{16,0},{32,16},{48,32},{64,48},{80,64},{96,80},{112,96},{0,112},{1... | collective-permute-start | bytes 98312 | tf_op jit(solution)/shard_map/ppermute | solution.py:459
  6.9 46.2 %copy-start = (s32[128]{0:T(128)S(1)}, s32[128]{0:T(128)}, u32[]{:S(2)}) copy-start(s32[128]{0:T(128)} %refs_0_.1) | copy-start | bytes 1540
  6.9 46.2 %copy-start.1 = (s32[128]{0:T(128)S(1)}, s32[128]{0:T(128)}, u32[]{:S(2)}) copy-start(s32[128]{0:T(128)} %refs_1_.1) | copy-start | bytes 1540

commit v6 on v5

--- a/solution.py
+++ b/solution.py
@@ -50,33 +50,45 @@
     return register % 3 + 3 * piece + (K if register >= 3 else 0)
 
 
-def edges_kernel(planes, head_ref, tail_ref):
-    shape = head_ref.shape
+def plane_of(planes, mask, mixed, p, rows, columns):
+    if p < 2 * K:
+        return planes[p, rows, columns]
+    return (mask if p == 2 * K else mixed)[rows, columns].astype(jnp.float32)
+
+
+def edges_kernel(planes, mask, mixed, near_ref, far_ref):
+    shape = near_ref.shape
     lane = lane_of(shape)
     last = planes.shape[2] - LANES
-    for start, edge, out_ref in ((0, 0, head_ref), (last, LANES - HALO, tail_ref)):
+    sides = []
+    for start, edge in ((0, 0), (last, LANES - HALO)):
         out = jnp.zeros(shape, jnp.float32)
         for p in range(PLANES):
             at = HALO * p
-            plane = rolled(planes[p, :, start : start + LANES], at - edge)
+            plane = plane_of(planes, mask, mixed, p, slice(None), slice(start, start + LANES))
+            plane = rolled(plane, at - edge)
             out = jnp.where((lane >= at) & (lane < at + HALO), plane, out)
-        out_ref[...] = out
-
-
-def edges(planes):
+        sides.append(out)
+    head, tail = sides
+    even = lax.axis_index("gx") % 2 == 0
+    near_ref[...] = jnp.where(even, tail, head)
+    far_ref[...] = jnp.where(even, head, tail)
+
+
+def edges(planes, mask, mixed):
     whole = pl.BlockSpec(memory_space=pltpu.VMEM)
     out = jax.ShapeDtypeStruct((planes.shape[1], LANES), jnp.float32)
     return pl.pallas_call(
         edges_kernel,
         out_shape=(out, out),
-        in_specs=[whole],
+        in_specs=[whole, whole, whole],
         out_specs=(whole, whole),
         compiler_params=pltpu.CompilerParams(vmem_limit_bytes=SMALL),
         name="edges",
-    )(planes)
-
-
-def pack_kernel(width, planes, out_ref):
+    )(planes, mask, mixed)
+
+
+def pack_kernel(width, planes, mask, mixed, out_ref):
     piece = width + 2 * HALO
     per_tile = LANES // width
     tiles = planes.shape[2] // LANES
@@ -95,7 +107,14 @@
             for m in range(SLOTS):
                 own = [
                     rolled(
-                        planes[plane_at(v, m), BR * b : BR * (b + 1), LANES * t : LANES * (t + 1)],
+                        plane_of(
+                            planes,
+                            mask,
+                            mixed,
+                            plane_at(v, m),
+                            slice(BR * b, BR * (b + 1)),
+                            slice(LANES * t, LANES * (t + 1)),
+                        ),
                         piece * m,
                     )
                     for t in range(tiles)
@@ -117,7 +136,7 @@
                 out_ref[j, b * VREGS + v] = jnp.where(one[q], parts[0], jnp.where(two[q], parts[1], parts[2]))
 
 
-def pack(planes, strips):
+def pack(planes, mask, mixed, strips):
     rows, columns = planes.shape[1:]
     whole = pl.BlockSpec(memory_space=pltpu.VMEM)
     width = columns // strips
@@ -128,21 +147,23 @@
     return pl.pallas_call(
         kernel,
         out_shape=jax.ShapeDtypeStruct((strips, rows // BR * VREGS, BR, LANES), jnp.float32),
-        in_specs=[whole],
+        in_specs=[whole, whole, whole],
         out_specs=whole,
         compiler_params=pltpu.CompilerParams(vmem_limit_bytes=SMALL),
         cost_estimate=pl.CostEstimate(flops=20000000, bytes_accessed=6000000, transcendentals=0),
         name="pack",
-    )(planes)
-
-
-def patch_kernel(width, west, east, packed, out_ref):
+    )(planes, mask, mixed)
+
+
+def patch_kernel(width, near, far, packed, out_ref):
     piece = width + 2 * HALO
+    even = lax.axis_index("gx") % 2 == 0
     lane = lane_of()
     strips = packed.shape[0]
 
-    def fill(b, strip, edge, start):
-        rim = edge[BR * b : BR * (b + 1), :]
+    def fill(b, strip, evens, odds, start):
+        here = slice(BR * b, BR * (b + 1))
+        rim = jnp.where(even, evens[here, :], odds[here, :])
         for v in range(VREGS):
             value = packed[strip, b * VREGS + v]
             for m in range(SLOTS):
@@ -151,12 +172,12 @@
                 value = jnp.where(here, rolled(rim, at - HALO * plane_at(v, m)), value)
             out_ref[strip, b * VREGS + v] = value
 
-    for b in range(west.shape[0] // BR):
-        fill(b, 0, west, LANES - HALO)
-        fill(b, strips - 1, east, 0)
-
-
-def patch(west, east, packed, width):
+    for b in range(near.shape[0] // BR):
+        fill(b, 0, far, near, LANES - HALO)
+        fill(b, strips - 1, near, far, 0)
+
+
+def patch(near, far, packed, width):
     whole = pl.BlockSpec(memory_space=pltpu.VMEM)
 
     def kernel(*refs):
@@ -170,7 +191,7 @@
         input_output_aliases={2: 0},
         compiler_params=pltpu.CompilerParams(vmem_limit_bytes=SMALL),
         name="patch",
-    )(west, east, packed)
+    )(near, far, packed)
 
 
 def sweep_kernel(
@@ -452,13 +473,12 @@
     ring = lax.axis_size("gx")
     width = columns // strips
     blocks = rows // BR
-    flats = [flat[None].astype(jnp.float32) for flat in (sea_mask, mixed_level)]
-    planes = jnp.concatenate([density, tracer, *flats])
-    head, tail = edges(planes)
-    west = lax.ppermute(tail, "gx", [(i, (i + 1) % ring) for i in range(ring)])
-    east = lax.ppermute(head, "gx", [((i + 1) % ring, i) for i in range(ring)])
-    packed = pack(planes, strips)
-    packed = patch(west, east, packed, width)
+    planes = jnp.concatenate([density, tracer])
+    near, far = edges(planes, sea_mask, mixed_level)
+    near = lax.ppermute(near, "gx", [(i, i ^ 1) for i in range(ring)])
+    far = lax.ppermute(far, "gx", [(i, (((i + 1) ^ 1) - 1) % ring) for i in range(ring)])
+    packed = pack(planes, sea_mask, mixed_level, strips)
+    packed = patch(near, far, packed, width)
     got = lax.all_to_all(packed, "gy", split_axis=0, concat_axis=0, tiled=True)
     done = sweeps(tile_blocks, block_owner, got.reshape(strips * blocks, VREGS, BR, LANES), width)
     back = lax.all_to_all(

time: 90.4 us -> 89.3 us (0.988); the launches traced: 90 us -> 87.7 us
  other arithmetic: 2.73 us -> 0 us
  waiting for transfers between devices: 1.02 us -> 2.75 us
  local copies, waits for them, and re-layouts: 0.01 us -> 1.62 us
  starting transfers between devices: 1.75 us -> 0.18 us
  blocking collectives: 68.2 us -> 66.8 us
    all_to_all x1, blocking collectives: 22 us -> 19.8 us  [on_device(): lax.all_to_all(done.reshape(strips, -1, BR, LANES), 'gy', split_axis=0, c...]
    concatenate x1 -> x0, other arithmetic: 1.75 us -> none  [on_device(): planes = jnp.concatenate([density, tracer, *flats])]
    ppermute x2, waiting for transfers between devices: 1.02 us -> 2.75 us  [the longest x1 2.22 us: on_device(): lax.ppermute(far, 'gx', [(i, ((i + 1 ^ 1) - 1) % ring) for i in range(rin...]
    ppermute x2, starting transfers between devices: 1.75 us -> 0.18 us  [the longest x1 0.1 us: on_device(): lax.ppermute(far, 'gx', [(i, ((i + 1 ^ 1) - 1) % ring) for i in range(rin...]
    unnamed x4 -> x11, local copies, waits for them, and re-layouts: 0.01 us -> 1.55 us
    convert_element_type x1 -> x0, other arithmetic: 0.99 us -> none  [on_device(): flats = [flat[None].astype(jnp.float32) for flat in (sea_mask, mixed_level)]]
  transfers between devices with their start and end apart: 2 -> 2, of which waited for: 1 -> 2; matrix products, arithmetic and copies ran while one was open for 0% -> 0% of each run, Pallas kernels for 1% -> 1%
where the time goes in v6:
time: 89.3 us; the launch traced here: 87.7 us
  blocking collectives  66.8 us (75%)
  Pallas kernels  16.2 us (18%)
  waiting for transfers between devices  2.75 us (3%)
  local copies, waits for them, and re-layouts  1.62 us (2%)
    all_to_all x1, blocking collectives, on_device(): got = lax.all_to_all(packed, 'gy', split_axis=0, concat_axis=0, tiled=True)  47 us
    all_to_all x1, blocking collectives, on_device(): lax.all_to_all(done.reshape(strips, -1, BR, LANES), 'gy', split_axis=0, c...  19.8 us
    pallas_call x1, Pallas kernels, sweeps(): pl.pallas_call(kernel, out_shape=jax.ShapeDtypeStruct((blocks, outs, BR,...  13.7 us
    ppermute x1, waiting for transfers between devices, on_device(): lax.ppermute(far, 'gx', [(i, ((i + 1 ^ 1) - 1) % ring) for i in range(rin...  2.22 us
  transfers between devices with their start and end apart: 2, of which 2 were waited for; matrix products, arithmetic and copies ran while one was open for 0% of the time, Pallas kernels for 1%

profile of v6, /device:TPU:32, one launch (start us, length us, event | category | flops | bytes accessed | tf_op | source)
XLA Modules:
  0.0 87.7 jit_solution(5732271582728468128)
XLA Ops:
  0.0 0.0 copy-start.4
  0.0 0.0 copy-start.1
  0.0 0.0 copy-start
  0.0 1.4 %constant_dynamic-update-slice_fusion.1 = f32[16,64,512]{2,1,0:T(8,128)S(1)} fusion(f32[8,64,512]{2,1,0:T(8,128)} %param.6), kind=kLoop, calls=%fused_computation.1 | loop fusion | bytes 2097152
  1.4 0.1 copy-done.4
  1.5 0.1 constant_dynamic-update-slice_fusion.planes.refs_0_
  1.6 0.0 copy-done.1
  1.6 0.0 copy-done
  1.6 0.4 edges.1
  2.0 0.1 collective-permute-start
  2.1 0.1 collective-permute-start.1
  2.2 0.6 pack.1.refs_2_
  2.8 0.5 collective-permute-done.refs_0_
  3.3 2.2 %collective-permute-done.1.refs_1_ = f32[64,128]{1,0:T(8,128)S(1)} collective-permute-done((f32[64,128]{1,0:T(8,128)S(1)}, f32[64,128]{1,0:T(8,128)S(1)}, u32[]{:S(2)}, u32[]{:S(2)}) %collective-permute-start.1) | collective-permute-done | bytes 32800 | tf_op jit(solution)/shard_map/ppermute | solution.py:479
  5.5 0.4 patch.1
  6.0 0.0 copy-start.2
  6.0 0.0 copy-start.3
  6.0 47.0 %all_to_all.10 = f32[16,48,8,128]{3,2,1,0:T(8,128)S(1)} all-to-all(f32[16,48,8,128]{3,2,1,0:T(8,128)S(1)} %patch.1), channel_id=1, replica_groups=mesh['gx'=8,'gy'=16] {'gy'}, dimensions={0} | all-to-all | bytes 6291456 | tf_op jit(solution)/shard_map/all_to_all | solution.py:482
  53.0 0.0 copy-done.2
  53.0 0.0 copy-done.3
  53.0 13.7 %sweeps.1 = f32[128,2,8,128]{3,2,1,0:T(8,128)S(1)} custom-call(s32[128]{0:T(128)S(1)} %copy-done.2, s32[128]{0:T(128)S(1)} %copy-done.3, f32[128,6,8,128]{3,2,1,0:T(8,128)S(1)} %bitcast.2), custom_call_target="tpu_custom_call" | custom-call | tf_op jit(solution)/shard_map/sweeps/pallas_call | solution.py:416
  66.7 19.8 %all_to_all.11.refs_0_ = f32[16,16,8,128]{3,2,1,0:T(8,128)S(1)} all-to-all(f32[16,16,8,128]{3,2,1,0:T(8,128)S(1)} %bitcast.3), channel_id=1, replica_groups=mesh['gx'=8,'gy'=16] {'gy'}, dimensions={0} | all-to-all | bytes 2097152 | tf_op jit(solution)/shard_map/all_to_all | solution.py:484
  86.5 1.1 %unpack.1 = f32[8,64,512]{2,1,0:T(8,128)} custom-call(f32[16,16,8,128]{3,2,1,0:T(8,128)S(1)} %all_to_all.11.refs_0_), custom_call_target="tpu_custom_call" | custom-call | tf_op jit(solution)/shard_map/unpack/pallas_call | solution.py:459
Async XLA Ops:
  0.0 1.5 %copy-start.4 = (f32[8,64,512]{2,1,0:T(8,128)S(1)}, f32[8,64,512]{2,1,0:T(8,128)}, u32[]{:S(2)}) copy-start(f32[8,64,512]{2,1,0:T(8,128)} %param.7) | copy-start | bytes 3145732
  0.0 1.6 %copy-start.1 = (s32[64,512]{1,0:T(8,128)S(1)}, s32[64,512]{1,0:T(8,128)}, u32[]{:S(2)}) copy-start(s32[64,512]{1,0:T(8,128)} %refs_2_.1) | copy-start | bytes 393220
  0.0 1.6 %copy-start = (s32[64,512]{1,0:T(8,128)S(1)}, s32[64,512]{1,0:T(8,128)}, u32[]{:S(2)}) copy-start(s32[64,512]{1,0:T(8,128)} %refs_1_.2) | copy-start | bytes 393220
  2.0 1.3 %collective-permute-start = (f32[64,128]{1,0:T(8,128)S(1)}, f32[64,128]{1,0:T(8,128)S(1)}, u32[]{:S(2)}, u32[]{:S(2)}) collective-permute-start(f32[64,128]{1,0:T(8,128)S(1)} %get-tuple-element.7), channel_id=1, source_target_pairs={{0,16},{16,0},{32,48},{48,32},{64,80},{80,64},{96,112},{112,96},{1... | collective-permute-start | bytes 98312 | tf_op jit(solution)/shard_map/ppermute | solution.py:478
  2.1 3.4 %collective-permute-start.1 = (f32[64,128]{1,0:T(8,128)S(1)}, f32[64,128]{1,0:T(8,128)S(1)}, u32[]{:S(2)}, u32[]{:S(2)}) collective-permute-start(f32[64,128]{1,0:T(8,128)S(1)} %get-tuple-element.8), channel_id=1, source_target_pairs={{0,112},{16,32},{32,16},{48,64},{64,48},{80,96},{96,80},{112,0},{1... | collective-permute-start | bytes 98312 | tf_op jit(solution)/shard_map/ppermute | solution.py:479
  6.0 47.0 %copy-start.2 = (s32[128]{0:T(128)S(1)}, s32[128]{0:T(128)}, u32[]{:S(2)}) copy-start(s32[128]{0:T(128)} %refs_0_.1) | copy-start | bytes 1540
  6.0 47.0 %copy-start.3 = (s32[128]{0:T(128)S(1)}, s32[128]{0:T(128)}, u32[]{:S(2)}) copy-start(s32[128]{0:T(128)} %refs_1_.3) | copy-start | bytes 1540

commit v7 on v6

--- a/solution.py
+++ b/solution.py
@@ -18,7 +18,6 @@
 UNIT = 4
 DEEPEST = 4
 GATHER = 4
-PHYSICS = 4
 FACES = 22
 SWEEP = 4
 LAST = 4
@@ -235,9 +234,6 @@
         ref[pl.ds(0, BR), :] = top
         ref[pl.ds(BR * (depth + 1), BR), :] = bottom
 
-    one = [lane_from(piece * n) < piece for n in range(SLOTS)]
-    two = [lane_from(piece * n) < 2 * piece for n in range(SLOTS)]
-
     def gather(c):
         for u in range(GATHER):
             i = c * GATHER + u
@@ -249,10 +245,9 @@
                 where = slots if v < 3 else owners
                 parts = [got[where[m], v] for m in range(SLOTS)]
                 parts[2] = parts[2] * real
-                parts = [rolled(parts[m], piece * m) for m in range(SLOTS)]
                 for n in range(SLOTS):
-                    plane = jnp.where(one[n], parts[0], jnp.where(two[n], parts[1], parts[2]))
-                    plane = rolled(plane, -piece * n)
+                    moved = [rolled(parts[m], piece * (m - n)) for m in range(SLOTS)]
+                    plane = jnp.where(first, moved[0], jnp.where(second, moved[1], moved[2]))
                     p = plane_at(v, n)
                     if p < K:
                         rho[p, at, :] = plane
@@ -262,17 +257,11 @@
                         sea[at, :] = plane
             levels = [got[slots[m], 5] for m in range(SLOTS)]
             levels[2] = levels[2] * real
-            levels = [rolled(levels[m], piece * m) for m in range(SLOTS)]
-            mix[at, :] = rolled(jnp.where(one[2], levels[0], jnp.where(two[2], levels[1], levels[2])), -2 * piece)
-
-    loop(gather, depth, GATHER)
-    for k in range(K):
-        close(rho.at[k])
-        close(ta.at[k])
-    close(sea)
+            levels = [rolled(levels[m], piece * (m - 2)) for m in range(SLOTS)]
+            mix[at, :] = jnp.where(first, levels[0], jnp.where(second, levels[1], levels[2]))
 
     def physics(c):
-        at, up, down = (rows(c, off, PHYSICS) for off in (0, 1, -1))
+        at, up, down = (rows(c, off, GATHER) for off in (0, 1, -1))
         mixed = mix[at, :]
         here = sea[at, :]
         east = rolled(here, -1) * here
@@ -316,7 +305,29 @@
             cq[k, at, :] = -weight * cq[k, at, :]
             cr[k, at, :] = (0.5 * weight) * kept[k]
 
-    loop(physics, depth, PHYSICS)
+    chunks = depth // GATHER
+
+    def opening(i, carry):
+        gather((i + chunks - 1) % chunks)
+        return carry
+
+    def both(c, carry):
+        physics(c)
+        gather(c + 2)
+        return carry
+
+    def closing(c, carry):
+        physics(c)
+        return carry
+
+    lax.fori_loop(0, 3, opening, 0)
+    for k in range(K):
+        close(rho.at[k])
+    close(sea)
+    lax.fori_loop(0, chunks - 3, both, 0)
+    lax.fori_loop(chunks - 3, chunks, closing, 0)
+    for k in range(K):
+        close(ta.at[k])
     close(kap)
 
     def faces(c):

time: 89.3 us -> 88.8 us (level)
  no operation moved by 1% of the time
where the time goes in v7:
time: 88.8 us; the launch traced here: 87.1 us
  blocking collectives  66.8 us (75%)
  Pallas kernels  15.7 us (18%)
  waiting for transfers between devices  2.75 us (3%)
  local copies, waits for them, and re-layouts  1.62 us (2%)
    all_to_all x1, blocking collectives, on_device(): got = lax.all_to_all(packed, 'gy', split_axis=0, concat_axis=0, tiled=True)  47 us
    all_to_all x1, blocking collectives, on_device(): lax.all_to_all(done.reshape(strips, -1, BR, LANES), 'gy', split_axis=0, c...  19.8 us
    pallas_call x1, Pallas kernels, sweeps(): pl.pallas_call(kernel, out_shape=jax.ShapeDtypeStruct((blocks, outs, BR,...  13.2 us
    ppermute x1, waiting for transfers between devices, on_device(): lax.ppermute(far, 'gx', [(i, ((i + 1 ^ 1) - 1) % ring) for i in range(rin...  2.22 us
  transfers between devices with their start and end apart: 2, of which 2 were waited for; matrix products, arithmetic and copies ran while one was open for 0% of the time, Pallas kernels for 1%

profile of v7, /device:TPU:32, one launch (start us, length us, event | category | flops | bytes accessed | tf_op | source)
XLA Modules:
  0.0 87.1 jit_solution(4531123235807454228)
XLA Ops:
  0.0 0.0 copy-start.4
  0.0 0.0 copy-start.1
  0.0 0.0 copy-start
  0.0 1.4 %constant_dynamic-update-slice_fusion.1 = f32[16,64,512]{2,1,0:T(8,128)S(1)} fusion(f32[8,64,512]{2,1,0:T(8,128)} %param.6), kind=kLoop, calls=%fused_computation.1 | loop fusion | bytes 2097152
  1.4 0.1 copy-done.4
  1.5 0.1 constant_dynamic-update-slice_fusion.planes.refs_0_
  1.6 0.0 copy-done.1
  1.6 0.0 copy-done
  1.6 0.4 edges.1
  2.0 0.1 collective-permute-start
  2.1 0.1 collective-permute-start.1
  2.2 0.6 pack.1.refs_2_
  2.8 0.5 collective-permute-done.refs_0_
  3.3 2.2 %collective-permute-done.1.refs_1_ = f32[64,128]{1,0:T(8,128)S(1)} collective-permute-done((f32[64,128]{1,0:T(8,128)S(1)}, f32[64,128]{1,0:T(8,128)S(1)}, u32[]{:S(2)}, u32[]{:S(2)}) %collective-permute-start.1) | collective-permute-done | bytes 32800 | tf_op jit(solution)/shard_map/ppermute | solution.py:490
  5.5 0.4 patch.1
  6.0 0.0 copy-start.2
  6.0 0.0 copy-start.3
  6.0 47.0 %all_to_all.10 = f32[16,48,8,128]{3,2,1,0:T(8,128)S(1)} all-to-all(f32[16,48,8,128]{3,2,1,0:T(8,128)S(1)} %patch.1), channel_id=1, replica_groups=mesh['gx'=8,'gy'=16] {'gy'}, dimensions={0} | all-to-all | bytes 6291456 | tf_op jit(solution)/shard_map/all_to_all | solution.py:493
  53.0 0.0 copy-done.2
  53.0 0.0 copy-done.3
  53.0 13.2 %sweeps.1 = f32[128,2,8,128]{3,2,1,0:T(8,128)S(1)} custom-call(s32[128]{0:T(128)S(1)} %copy-done.2, s32[128]{0:T(128)S(1)} %copy-done.3, f32[128,6,8,128]{3,2,1,0:T(8,128)S(1)} %bitcast.2), custom_call_target="tpu_custom_call" | custom-call | tf_op jit(solution)/shard_map/sweeps/pallas_call | solution.py:427
  66.2 19.8 %all_to_all.11.refs_0_ = f32[16,16,8,128]{3,2,1,0:T(8,128)S(1)} all-to-all(f32[16,16,8,128]{3,2,1,0:T(8,128)S(1)} %bitcast.3), channel_id=1, replica_groups=mesh['gx'=8,'gy'=16] {'gy'}, dimensions={0} | all-to-all | bytes 2097152 | tf_op jit(solution)/shard_map/all_to_all | solution.py:495
  86.0 1.1 %unpack.1 = f32[8,64,512]{2,1,0:T(8,128)} custom-call(f32[16,16,8,128]{3,2,1,0:T(8,128)S(1)} %all_to_all.11.refs_0_), custom_call_target="tpu_custom_call" | custom-call | tf_op jit(solution)/shard_map/unpack/pallas_call | solution.py:470
Async XLA Ops:
  0.0 1.5 %copy-start.4 = (f32[8,64,512]{2,1,0:T(8,128)S(1)}, f32[8,64,512]{2,1,0:T(8,128)}, u32[]{:S(2)}) copy-start(f32[8,64,512]{2,1,0:T(8,128)} %param.7) | copy-start | bytes 3145732
  0.0 1.6 %copy-start.1 = (s32[64,512]{1,0:T(8,128)S(1)}, s32[64,512]{1,0:T(8,128)}, u32[]{:S(2)}) copy-start(s32[64,512]{1,0:T(8,128)} %refs_2_.1) | copy-start | bytes 393220
  0.0 1.6 %copy-start = (s32[64,512]{1,0:T(8,128)S(1)}, s32[64,512]{1,0:T(8,128)}, u32[]{:S(2)}) copy-start(s32[64,512]{1,0:T(8,128)} %refs_1_.2) | copy-start | bytes 393220
  2.0 1.3 %collective-permute-start = (f32[64,128]{1,0:T(8,128)S(1)}, f32[64,128]{1,0:T(8,128)S(1)}, u32[]{:S(2)}, u32[]{:S(2)}) collective-permute-start(f32[64,128]{1,0:T(8,128)S(1)} %get-tuple-element.7), channel_id=1, source_target_pairs={{0,16},{16,0},{32,48},{48,32},{64,80},{80,64},{96,112},{112,96},{1... | collective-permute-start | bytes 98312 | tf_op jit(solution)/shard_map/ppermute | solution.py:489
  2.1 3.4 %collective-permute-start.1 = (f32[64,128]{1,0:T(8,128)S(1)}, f32[64,128]{1,0:T(8,128)S(1)}, u32[]{:S(2)}, u32[]{:S(2)}) collective-permute-start(f32[64,128]{1,0:T(8,128)S(1)} %get-tuple-element.8), channel_id=1, source_target_pairs={{0,112},{16,32},{32,16},{48,64},{64,48},{80,96},{96,80},{112,0},{1... | collective-permute-start | bytes 98312 | tf_op jit(solution)/shard_map/ppermute | solution.py:490
  6.0 47.0 %copy-start.2 = (s32[128]{0:T(128)S(1)}, s32[128]{0:T(128)}, u32[]{:S(2)}) copy-start(s32[128]{0:T(128)} %refs_0_.1) | copy-start | bytes 1540
  6.0 47.0 %copy-start.3 = (s32[128]{0:T(128)S(1)}, s32[128]{0:T(128)}, u32[]{:S(2)}) copy-start(s32[128]{0:T(128)} %refs_1_.3) | copy-start | bytes 1540

commit v8 on v7

--- a/solution.py
+++ b/solution.py
@@ -18,7 +18,7 @@
 UNIT = 4
 DEEPEST = 4
 GATHER = 4
-FACES = 22
+FACES = 44
 SWEEP = 4
 LAST = 4
 

time: 88.8 us -> 88.6 us (level)
  no operation moved by 1% of the time
where the time goes in v8:
time: 88.6 us; the launch traced here: 87 us
  blocking collectives  66.8 us (75%)
  Pallas kernels  15.5 us (17%)
  waiting for transfers between devices  2.75 us (3%)
  local copies, waits for them, and re-layouts  1.62 us (2%)
    all_to_all x1, blocking collectives, on_device(): got = lax.all_to_all(packed, 'gy', split_axis=0, concat_axis=0, tiled=True)  47 us
    all_to_all x1, blocking collectives, on_device(): lax.all_to_all(done.reshape(strips, -1, BR, LANES), 'gy', split_axis=0, c...  19.8 us
    pallas_call x1, Pallas kernels, sweeps(): pl.pallas_call(kernel, out_shape=jax.ShapeDtypeStruct((blocks, outs, BR,...  13 us
    ppermute x1, waiting for transfers between devices, on_device(): lax.ppermute(far, 'gx', [(i, ((i + 1 ^ 1) - 1) % ring) for i in range(rin...  2.22 us
  transfers between devices with their start and end apart: 2, of which 2 were waited for; matrix products, arithmetic and copies ran while one was open for 0% of the time, Pallas kernels for 1%

profile of v8, /device:TPU:32, one launch (start us, length us, event | category | flops | bytes accessed | tf_op | source)
XLA Modules:
  0.0 87.0 jit_solution(8812284795457205886)
XLA Ops:
  0.0 0.0 copy-start.4
  0.0 0.0 copy-start.1
  0.0 0.0 copy-start
  0.0 1.4 %constant_dynamic-update-slice_fusion.1 = f32[16,64,512]{2,1,0:T(8,128)S(1)} fusion(f32[8,64,512]{2,1,0:T(8,128)} %param.6), kind=kLoop, calls=%fused_computation.1 | loop fusion | bytes 2097152
  1.4 0.1 copy-done.4
  1.5 0.1 constant_dynamic-update-slice_fusion.planes.refs_0_
  1.6 0.0 copy-done.1
  1.6 0.0 copy-done
  1.6 0.4 edges.1
  2.0 0.1 collective-permute-start
  2.1 0.1 collective-permute-start.1
  2.2 0.6 pack.1.refs_2_
  2.8 0.5 collective-permute-done.refs_0_
  3.3 2.2 %collective-permute-done.1.refs_1_ = f32[64,128]{1,0:T(8,128)S(1)} collective-permute-done((f32[64,128]{1,0:T(8,128)S(1)}, f32[64,128]{1,0:T(8,128)S(1)}, u32[]{:S(2)}, u32[]{:S(2)}) %collective-permute-start.1) | collective-permute-done | bytes 32800 | tf_op jit(solution)/shard_map/ppermute | solution.py:490
  5.5 0.4 patch.1
  6.0 0.0 copy-start.2
  6.0 0.0 copy-start.3
  6.0 47.0 %all_to_all.10 = f32[16,48,8,128]{3,2,1,0:T(8,128)S(1)} all-to-all(f32[16,48,8,128]{3,2,1,0:T(8,128)S(1)} %patch.1), channel_id=1, replica_groups=mesh['gx'=8,'gy'=16] {'gy'}, dimensions={0} | all-to-all | bytes 6291456 | tf_op jit(solution)/shard_map/all_to_all | solution.py:493
  53.0 0.0 copy-done.2
  53.0 0.0 copy-done.3
  53.0 13.0 %sweeps.1 = f32[128,2,8,128]{3,2,1,0:T(8,128)S(1)} custom-call(s32[128]{0:T(128)S(1)} %copy-done.2, s32[128]{0:T(128)S(1)} %copy-done.3, f32[128,6,8,128]{3,2,1,0:T(8,128)S(1)} %bitcast.2), custom_call_target="tpu_custom_call" | custom-call | tf_op jit(solution)/shard_map/sweeps/pallas_call | solution.py:427
  66.0 19.8 %all_to_all.11.refs_0_ = f32[16,16,8,128]{3,2,1,0:T(8,128)S(1)} all-to-all(f32[16,16,8,128]{3,2,1,0:T(8,128)S(1)} %bitcast.3), channel_id=1, replica_groups=mesh['gx'=8,'gy'=16] {'gy'}, dimensions={0} | all-to-all | bytes 2097152 | tf_op jit(solution)/shard_map/all_to_all | solution.py:495
  85.8 1.1 %unpack.1 = f32[8,64,512]{2,1,0:T(8,128)} custom-call(f32[16,16,8,128]{3,2,1,0:T(8,128)S(1)} %all_to_all.11.refs_0_), custom_call_target="tpu_custom_call" | custom-call | tf_op jit(solution)/shard_map/unpack/pallas_call | solution.py:470
Async XLA Ops:
  0.0 1.5 %copy-start.4 = (f32[8,64,512]{2,1,0:T(8,128)S(1)}, f32[8,64,512]{2,1,0:T(8,128)}, u32[]{:S(2)}) copy-start(f32[8,64,512]{2,1,0:T(8,128)} %param.7) | copy-start | bytes 3145732
  0.0 1.6 %copy-start.1 = (s32[64,512]{1,0:T(8,128)S(1)}, s32[64,512]{1,0:T(8,128)}, u32[]{:S(2)}) copy-start(s32[64,512]{1,0:T(8,128)} %refs_2_.1) | copy-start | bytes 393220
  0.0 1.6 %copy-start = (s32[64,512]{1,0:T(8,128)S(1)}, s32[64,512]{1,0:T(8,128)}, u32[]{:S(2)}) copy-start(s32[64,512]{1,0:T(8,128)} %refs_1_.2) | copy-start | bytes 393220
  2.0 1.3 %collective-permute-start = (f32[64,128]{1,0:T(8,128)S(1)}, f32[64,128]{1,0:T(8,128)S(1)}, u32[]{:S(2)}, u32[]{:S(2)}) collective-permute-start(f32[64,128]{1,0:T(8,128)S(1)} %get-tuple-element.7), channel_id=1, source_target_pairs={{0,16},{16,0},{32,48},{48,32},{64,80},{80,64},{96,112},{112,96},{1... | collective-permute-start | bytes 98312 | tf_op jit(solution)/shard_map/ppermute | solution.py:489
  2.1 3.4 %collective-permute-start.1 = (f32[64,128]{1,0:T(8,128)S(1)}, f32[64,128]{1,0:T(8,128)S(1)}, u32[]{:S(2)}, u32[]{:S(2)}) collective-permute-start(f32[64,128]{1,0:T(8,128)S(1)} %get-tuple-element.8), channel_id=1, source_target_pairs={{0,112},{16,32},{32,16},{48,64},{64,48},{80,96},{96,80},{112,0},{1... | collective-permute-start | bytes 98312 | tf_op jit(solution)/shard_map/ppermute | solution.py:490
  6.0 47.0 %copy-start.2 = (s32[128]{0:T(128)S(1)}, s32[128]{0:T(128)}, u32[]{:S(2)}) copy-start(s32[128]{0:T(128)} %refs_0_.1) | copy-start | bytes 1540
  6.0 47.0 %copy-start.3 = (s32[128]{0:T(128)S(1)}, s32[128]{0:T(128)}, u32[]{:S(2)}) copy-start(s32[128]{0:T(128)} %refs_1_.3) | copy-start | bytes 1540

commit v9 on v8

--- a/solution.py
+++ b/solution.py
@@ -286,24 +286,24 @@
             se = sum_e * scale
             sn = sum_n * scale
             squared = se * se + sn * sn
-            taper = 0.5 + 0.5 * jnp.tanh(SLOPE_LIMIT / TAPER_WIDTH - squared * (1.0 / TAPER_WIDTH))
+            taper = 1.0 + jnp.tanh(SLOPE_LIMIT / TAPER_WIDTH - squared * (1.0 / TAPER_WIDTH))
             if k < DEEPEST:
                 taper = taper * jnp.minimum(1.0, (k + 1.0) * per_mixed)
             squared = squared * (taper * taper)
-            under_root = twice * (squared + KERNEL_OFFSET)
+            under_root = twice * (squared + 4.0 * KERNEL_OFFSET)
             root = under_root * lax.rsqrt(under_root)
             total += jnp.where(mixed <= float(k), root, 0.0) if k < DEEPEST else root
             cp[k, at, :] = se * taper
             cq[k, at, :] = sn * taper
             kept.append(squared)
-        share = (VISBECK_ALPHA * 0.5**0.5) * total / (K - mixed)
+        share = (0.5 * VISBECK_ALPHA * 0.5**0.5) * total / (K - mixed)
         kappa = here * (BASE_DIFFUSIVITY + share)
         kap[at, :] = kappa
-        weight = (0.5 * TIME_STEP) * kappa
+        weight = (0.25 * TIME_STEP) * kappa
         for k in range(K):
             cp[k, at, :] = -weight * cp[k, at, :]
             cq[k, at, :] = -weight * cq[k, at, :]
-            cr[k, at, :] = (0.5 * weight) * kept[k]
+            cr[k, at, :] = (0.25 * weight) * kept[k]
 
     chunks = depth // GATHER
 

time: 88.6 us -> 88.6 us (level)
  no operation moved by 1% of the time
where the time goes in v9:
time: 88.6 us; the launch traced here: 86.9 us
  blocking collectives  66.8 us (75%)
  Pallas kernels  15.5 us (17%)
  waiting for transfers between devices  2.75 us (3%)
  local copies, waits for them, and re-layouts  1.62 us (2%)
    all_to_all x1, blocking collectives, on_device(): got = lax.all_to_all(packed, 'gy', split_axis=0, concat_axis=0, tiled=True)  47 us
    all_to_all x1, blocking collectives, on_device(): lax.all_to_all(done.reshape(strips, -1, BR, LANES), 'gy', split_axis=0, c...  19.8 us
    pallas_call x1, Pallas kernels, sweeps(): pl.pallas_call(kernel, out_shape=jax.ShapeDtypeStruct((blocks, outs, BR,...  13 us
    ppermute x1, waiting for transfers between devices, on_device(): lax.ppermute(far, 'gx', [(i, ((i + 1 ^ 1) - 1) % ring) for i in range(rin...  2.22 us
  transfers between devices with their start and end apart: 2, of which 2 were waited for; matrix products, arithmetic and copies ran while one was open for 0% of the time, Pallas kernels for 1%

profile of v9, /device:TPU:32, one launch (start us, length us, event | category | flops | bytes accessed | tf_op | source)
XLA Modules:
  0.0 86.9 jit_solution(4956811648298000361)
XLA Ops:
  0.0 0.0 copy-start.4
  0.0 0.0 copy-start.1
  0.0 0.0 copy-start
  0.0 1.4 %constant_dynamic-update-slice_fusion.1 = f32[16,64,512]{2,1,0:T(8,128)S(1)} fusion(f32[8,64,512]{2,1,0:T(8,128)} %param.6), kind=kLoop, calls=%fused_computation.1 | loop fusion | bytes 2097152
  1.4 0.1 copy-done.4
  1.5 0.1 constant_dynamic-update-slice_fusion.planes.refs_0_
  1.6 0.0 copy-done.1
  1.6 0.0 copy-done
  1.6 0.4 edges.1
  2.0 0.1 collective-permute-start
  2.1 0.1 collective-permute-start.1
  2.2 0.6 pack.1.refs_2_
  2.8 0.5 collective-permute-done.refs_0_
  3.3 2.2 %collective-permute-done.1.refs_1_ = f32[64,128]{1,0:T(8,128)S(1)} collective-permute-done((f32[64,128]{1,0:T(8,128)S(1)}, f32[64,128]{1,0:T(8,128)S(1)}, u32[]{:S(2)}, u32[]{:S(2)}) %collective-permute-start.1) | collective-permute-done | bytes 32800 | tf_op jit(solution)/shard_map/ppermute | solution.py:490
  5.5 0.4 patch.1
  6.0 0.0 copy-start.2
  6.0 0.0 copy-start.3
  6.0 47.0 %all_to_all.10 = f32[16,48,8,128]{3,2,1,0:T(8,128)S(1)} all-to-all(f32[16,48,8,128]{3,2,1,0:T(8,128)S(1)} %patch.1), channel_id=1, replica_groups=mesh['gx'=8,'gy'=16] {'gy'}, dimensions={0} | all-to-all | bytes 6291456 | tf_op jit(solution)/shard_map/all_to_all | solution.py:493
  53.0 0.0 copy-done.2
  53.0 0.0 copy-done.3
  53.0 13.0 %sweeps.1 = f32[128,2,8,128]{3,2,1,0:T(8,128)S(1)} custom-call(s32[128]{0:T(128)S(1)} %copy-done.2, s32[128]{0:T(128)S(1)} %copy-done.3, f32[128,6,8,128]{3,2,1,0:T(8,128)S(1)} %bitcast.2), custom_call_target="tpu_custom_call" | custom-call | tf_op jit(solution)/shard_map/sweeps/pallas_call | solution.py:427
  66.0 19.8 %all_to_all.11.refs_0_ = f32[16,16,8,128]{3,2,1,0:T(8,128)S(1)} all-to-all(f32[16,16,8,128]{3,2,1,0:T(8,128)S(1)} %bitcast.3), channel_id=1, replica_groups=mesh['gx'=8,'gy'=16] {'gy'}, dimensions={0} | all-to-all | bytes 2097152 | tf_op jit(solution)/shard_map/all_to_all | solution.py:495
  85.8 1.1 %unpack.1 = f32[8,64,512]{2,1,0:T(8,128)} custom-call(f32[16,16,8,128]{3,2,1,0:T(8,128)S(1)} %all_to_all.11.refs_0_), custom_call_target="tpu_custom_call" | custom-call | tf_op jit(solution)/shard_map/unpack/pallas_call | solution.py:470
Async XLA Ops:
  0.0 1.5 %copy-start.4 = (f32[8,64,512]{2,1,0:T(8,128)S(1)}, f32[8,64,512]{2,1,0:T(8,128)}, u32[]{:S(2)}) copy-start(f32[8,64,512]{2,1,0:T(8,128)} %param.7) | copy-start | bytes 3145732
  0.0 1.6 %copy-start.1 = (s32[64,512]{1,0:T(8,128)S(1)}, s32[64,512]{1,0:T(8,128)}, u32[]{:S(2)}) copy-start(s32[64,512]{1,0:T(8,128)} %refs_2_.1) | copy-start | bytes 393220
  0.0 1.6 %copy-start = (s32[64,512]{1,0:T(8,128)S(1)}, s32[64,512]{1,0:T(8,128)}, u32[]{:S(2)}) copy-start(s32[64,512]{1,0:T(8,128)} %refs_1_.2) | copy-start | bytes 393220
  2.0 1.3 %collective-permute-start = (f32[64,128]{1,0:T(8,128)S(1)}, f32[64,128]{1,0:T(8,128)S(1)}, u32[]{:S(2)}, u32[]{:S(2)}) collective-permute-start(f32[64,128]{1,0:T(8,128)S(1)} %get-tuple-element.7), channel_id=1, source_target_pairs={{0,16},{16,0},{32,48},{48,32},{64,80},{80,64},{96,112},{112,96},{1... | collective-permute-start | bytes 98312 | tf_op jit(solution)/shard_map/ppermute | solution.py:489
  2.1 3.4 %collective-permute-start.1 = (f32[64,128]{1,0:T(8,128)S(1)}, f32[64,128]{1,0:T(8,128)S(1)}, u32[]{:S(2)}, u32[]{:S(2)}) collective-permute-start(f32[64,128]{1,0:T(8,128)S(1)} %get-tuple-element.8), channel_id=1, source_target_pairs={{0,112},{16,32},{32,16},{48,64},{64,48},{80,96},{96,80},{112,0},{1... | collective-permute-start | bytes 98312 | tf_op jit(solution)/shard_map/ppermute | solution.py:490
  6.0 47.0 %copy-start.2 = (s32[128]{0:T(128)S(1)}, s32[128]{0:T(128)}, u32[]{:S(2)}) copy-start(s32[128]{0:T(128)} %refs_0_.1) | copy-start | bytes 1540
  6.0 47.0 %copy-start.3 = (s32[128]{0:T(128)S(1)}, s32[128]{0:T(128)}, u32[]{:S(2)}) copy-start(s32[128]{0:T(128)} %refs_1_.3) | copy-start | bytes 1540

commit v10 on v9

--- a/solution.py
+++ b/solution.py
@@ -14,7 +14,7 @@
 VREGS = 6
 UNPACK = 2
 SMALL = 12 * 1024 * 1024
-PLANES = 2 * K + 2
+SPACING = 32 + 2 * HALO
 UNIT = 4
 DEEPEST = 4
 GATHER = 4
@@ -62,11 +62,12 @@
     sides = []
     for start, edge in ((0, 0), (last, LANES - HALO)):
         out = jnp.zeros(shape, jnp.float32)
-        for p in range(PLANES):
-            at = HALO * p
-            plane = plane_of(planes, mask, mixed, p, slice(None), slice(start, start + LANES))
-            plane = rolled(plane, at - edge)
-            out = jnp.where((lane >= at) & (lane < at + HALO), plane, out)
+        for v in range(VREGS):
+            for m in range(SLOTS):
+                at = SPACING * m + HALO * v
+                plane = plane_of(planes, mask, mixed, plane_at(v, m), slice(None), slice(start, start + LANES))
+                here = (lane >= at) & (lane < at + HALO)
+                out = jnp.where(here, rolled(plane, at - edge), out)
         sides.append(out)
     head, tail = sides
     even = lax.axis_index("gx") % 2 == 0
@@ -156,6 +157,7 @@
 
 def patch_kernel(width, near, far, packed, out_ref):
     piece = width + 2 * HALO
+    assert piece == SPACING
     even = lax.axis_index("gx") % 2 == 0
     lane = lane_of()
     strips = packed.shape[0]
@@ -163,13 +165,12 @@
     def fill(b, strip, evens, odds, start):
         here = slice(BR * b, BR * (b + 1))
         rim = jnp.where(even, evens[here, :], odds[here, :])
+        hole = ((lane - start) & (LANES - 1)) < HALO
+        for m in range(1, SLOTS):
+            hole |= ((lane - (piece * m + start)) & (LANES - 1)) < HALO
         for v in range(VREGS):
-            value = packed[strip, b * VREGS + v]
-            for m in range(SLOTS):
-                at = (piece * m + start) % LANES
-                here = (lane >= at) & (lane < at + HALO)
-                value = jnp.where(here, rolled(rim, at - HALO * plane_at(v, m)), value)
-            out_ref[strip, b * VREGS + v] = value
+            at = b * VREGS + v
+            out_ref[strip, at] = jnp.where(hole, rolled(rim, start - HALO * v), packed[strip, at])
 
     for b in range(near.shape[0] // BR):
         fill(b, 0, far, near, LANES - HALO)
@@ -273,15 +274,14 @@
         mn[at, :] = north
         ms[at, :] = south
         per_mixed = 1.0 / (mixed + 1.0)
-        f = [rho[k, at, :] for k in range(K)]
         total = jnp.zeros_like(here)
-        kept = []
         for k in range(K):
-            sum_e = east * (rolled(f[k], -1) - f[k]) + west * (f[k] - rolled(f[k], 1))
-            sum_n = north * (rho[k, up, :] - f[k]) + south * (f[k] - rho[k, down, :])
+            f = rho[k, at, :]
+            sum_e = east * (rolled(f, -1) - f) + west * (f - rolled(f, 1))
+            sum_n = north * (rho[k, up, :] - f) + south * (f - rho[k, down, :])
             above, under = max(k - 1, 0), min(k + 1, K - 1)
             rising = STRATIFICATION * (under - above)
-            twice = jnp.maximum((f[under] - f[above]) + rising, 2.0 * DENSITY_FLOOR)
+            twice = jnp.maximum((rho[under, at, :] - rho[above, at, :]) + rising, 2.0 * DENSITY_FLOOR)
             scale = 1.0 / twice
             se = sum_e * scale
             sn = sum_n * scale
@@ -295,7 +295,7 @@
             total += jnp.where(mixed <= float(k), root, 0.0) if k < DEEPEST else root
             cp[k, at, :] = se * taper
             cq[k, at, :] = sn * taper
-            kept.append(squared)
+            cr[k, at, :] = squared
         share = (0.5 * VISBECK_ALPHA * 0.5**0.5) * total / (K - mixed)
         kappa = here * (BASE_DIFFUSIVITY + share)
         kap[at, :] = kappa
@@ -303,7 +303,7 @@
         for k in range(K):
             cp[k, at, :] = -weight * cp[k, at, :]
             cq[k, at, :] = -weight * cq[k, at, :]
-            cr[k, at, :] = (0.25 * weight) * kept[k]
+            cr[k, at, :] = (0.25 * weight) * cr[k, at, :]
 
     chunks = depth // GATHER
 

time: 88.6 us -> 88.3 us (level)
  no operation moved by 1% of the time
where the time goes in v10:
time: 88.3 us; the launch traced here: 86.6 us
  blocking collectives  66.8 us (76%)
  Pallas kernels  15.1 us (17%)
  waiting for transfers between devices  2.75 us (3%)
  local copies, waits for them, and re-layouts  1.62 us (2%)
    all_to_all x1, blocking collectives, on_device(): got = lax.all_to_all(packed, 'gy', split_axis=0, concat_axis=0, tiled=True)  47 us
    all_to_all x1, blocking collectives, on_device(): lax.all_to_all(done.reshape(strips, -1, BR, LANES), 'gy', split_axis=0, c...  19.8 us
    pallas_call x1, Pallas kernels, sweeps(): pl.pallas_call(kernel, out_shape=jax.ShapeDtypeStruct((blocks, outs, BR,...  12.9 us
    ppermute x1, waiting for transfers between devices, on_device(): lax.ppermute(far, 'gx', [(i, ((i + 1 ^ 1) - 1) % ring) for i in range(rin...  2.22 us
  transfers between devices with their start and end apart: 2, of which 2 were waited for; matrix products, arithmetic and copies ran while one was open for 0% of the time, Pallas kernels for 1%

profile of v10, /device:TPU:32, one launch (start us, length us, event | category | flops | bytes accessed | tf_op | source)
XLA Modules:
  0.0 86.6 jit_solution(12615535115703808549)
XLA Ops:
  0.0 0.0 copy-start.4
  0.0 0.0 copy-start.1
  0.0 0.0 copy-start
  0.0 1.4 %constant_dynamic-update-slice_fusion.1 = f32[16,64,512]{2,1,0:T(8,128)S(1)} fusion(f32[8,64,512]{2,1,0:T(8,128)} %param.6), kind=kLoop, calls=%fused_computation.1 | loop fusion | bytes 2097152
  1.4 0.1 copy-done.4
  1.5 0.1 constant_dynamic-update-slice_fusion.planes.refs_0_
  1.6 0.0 copy-done.1
  1.6 0.0 copy-done
  1.6 0.4 edges.1
  2.0 0.1 collective-permute-start
  2.1 0.1 collective-permute-start.1
  2.2 0.6 pack.1.refs_2_
  2.8 0.5 collective-permute-done.refs_0_
  3.3 2.2 %collective-permute-done.1.refs_1_ = f32[64,128]{1,0:T(8,128)S(1)} collective-permute-done((f32[64,128]{1,0:T(8,128)S(1)}, f32[64,128]{1,0:T(8,128)S(1)}, u32[]{:S(2)}, u32[]{:S(2)}) %collective-permute-start.1) | collective-permute-done | bytes 32800 | tf_op jit(solution)/shard_map/ppermute | solution.py:490
  5.5 0.2 patch.1
  5.7 0.0 copy-start.2
  5.7 0.0 copy-start.3
  5.7 47.0 %all_to_all.10 = f32[16,48,8,128]{3,2,1,0:T(8,128)S(1)} all-to-all(f32[16,48,8,128]{3,2,1,0:T(8,128)S(1)} %patch.1), channel_id=1, replica_groups=mesh['gx'=8,'gy'=16] {'gy'}, dimensions={0} | all-to-all | bytes 6291456 | tf_op jit(solution)/shard_map/all_to_all | solution.py:493
  52.7 0.0 copy-done.2
  52.7 0.0 copy-done.3
  52.7 12.9 %sweeps.1 = f32[128,2,8,128]{3,2,1,0:T(8,128)S(1)} custom-call(s32[128]{0:T(128)S(1)} %copy-done.2, s32[128]{0:T(128)S(1)} %copy-done.3, f32[128,6,8,128]{3,2,1,0:T(8,128)S(1)} %bitcast.2), custom_call_target="tpu_custom_call" | custom-call | tf_op jit(solution)/shard_map/sweeps/pallas_call | solution.py:427
  65.6 19.8 %all_to_all.11.refs_0_ = f32[16,16,8,128]{3,2,1,0:T(8,128)S(1)} all-to-all(f32[16,16,8,128]{3,2,1,0:T(8,128)S(1)} %bitcast.3), channel_id=1, replica_groups=mesh['gx'=8,'gy'=16] {'gy'}, dimensions={0} | all-to-all | bytes 2097152 | tf_op jit(solution)/shard_map/all_to_all | solution.py:495
  85.4 1.1 %unpack.1 = f32[8,64,512]{2,1,0:T(8,128)} custom-call(f32[16,16,8,128]{3,2,1,0:T(8,128)S(1)} %all_to_all.11.refs_0_), custom_call_target="tpu_custom_call" | custom-call | tf_op jit(solution)/shard_map/unpack/pallas_call | solution.py:470
Async XLA Ops:
  0.0 1.5 %copy-start.4 = (f32[8,64,512]{2,1,0:T(8,128)S(1)}, f32[8,64,512]{2,1,0:T(8,128)}, u32[]{:S(2)}) copy-start(f32[8,64,512]{2,1,0:T(8,128)} %param.7) | copy-start | bytes 3145732
  0.0 1.6 %copy-start.1 = (s32[64,512]{1,0:T(8,128)S(1)}, s32[64,512]{1,0:T(8,128)}, u32[]{:S(2)}) copy-start(s32[64,512]{1,0:T(8,128)} %refs_2_.1) | copy-start | bytes 393220
  0.0 1.6 %copy-start = (s32[64,512]{1,0:T(8,128)S(1)}, s32[64,512]{1,0:T(8,128)}, u32[]{:S(2)}) copy-start(s32[64,512]{1,0:T(8,128)} %refs_1_.2) | copy-start | bytes 393220
  2.0 1.3 %collective-permute-start = (f32[64,128]{1,0:T(8,128)S(1)}, f32[64,128]{1,0:T(8,128)S(1)}, u32[]{:S(2)}, u32[]{:S(2)}) collective-permute-start(f32[64,128]{1,0:T(8,128)S(1)} %get-tuple-element.7), channel_id=1, source_target_pairs={{0,16},{16,0},{32,48},{48,32},{64,80},{80,64},{96,112},{112,96},{1... | collective-permute-start | bytes 98312 | tf_op jit(solution)/shard_map/ppermute | solution.py:489
  2.1 3.4 %collective-permute-start.1 = (f32[64,128]{1,0:T(8,128)S(1)}, f32[64,128]{1,0:T(8,128)S(1)}, u32[]{:S(2)}, u32[]{:S(2)}) collective-permute-start(f32[64,128]{1,0:T(8,128)S(1)} %get-tuple-element.8), channel_id=1, source_target_pairs={{0,112},{16,32},{32,16},{48,64},{64,48},{80,96},{96,80},{112,0},{1... | collective-permute-start | bytes 98312 | tf_op jit(solution)/shard_map/ppermute | solution.py:490
  5.7 47.0 %copy-start.2 = (s32[128]{0:T(128)S(1)}, s32[128]{0:T(128)}, u32[]{:S(2)}) copy-start(s32[128]{0:T(128)} %refs_0_.1) | copy-start | bytes 1540
  5.7 47.0 %copy-start.3 = (s32[128]{0:T(128)S(1)}, s32[128]{0:T(128)}, u32[]{:S(2)}) copy-start(s32[128]{0:T(128)} %refs_1_.3) | copy-start | bytes 1540
